TPU v7x, 128 devices: a whole 4x4x4 slice. The times are simulated.
128 devices in a mesh: batch: 4 (over z), seq: 16 (over y, x_lo, core), head: 2 (over x_hi).
Axes of the slice: x: 4 (x_hi: 2, x_lo: 2; x = x_hi * 2 + x_lo), y: 4, z: 4, core: 2. Of those that a mesh axis runs over, the one named last changes fastest.
Arguments:
- image_hidden: bfloat16 [8, 4096, 3072], P('batch', 'seq', 'head'), parts along dimension 0, may hold values from -6 to 6
- modulation: float32 [8, 3, 3072], P('batch'), parts along dimension 0, may hold values from -4 to 4
- qkv_weight: bfloat16 [3072, 3, 1536], P(None, None, 'head'), may hold values from -0.109375 to 0.109375
- out_weight: bfloat16 [1536, 3072], P('head'), may hold values from -0.15625 to 0.15625
- q_gain: float32 [128], replicated, may hold values from 1.2 to 2.5
- k_gain: float32 [128], replicated, may hold values from 1.2 to 2.5
- text_keys: bfloat16 [8, 512, 1536], P('batch', 'seq', 'head'), parts along dimension 0, may hold values from -10 to 10
- text_values: bfloat16 [8, 512, 1536], P('batch', 'seq', 'head'), parts along dimension 0, may hold values from -6 to 6
- stale_keys: bfloat16 [8, 4096, 1536], P('batch', 'seq', 'head'), parts along dimension 0, may hold values from -64 to 64
- stale_values: bfloat16 [8, 4096, 1536], P('batch', 'seq', 'head'), parts along dimension 0, may hold values from -6 to 6
- cached_residual: bfloat16 [8, 4096, 3072], P('batch', 'seq', 'head'), parts along dimension 0, may hold values from -6 to 6
- patch_of: int32 [64], P('batch'), parts along dimension 0, may hold values from 0 to 15, each once
- refresh: int32 [64], P('batch'), parts along dimension 0, may hold values from 0 to 1, as said below
- text_len: int32 [8], P('batch'), parts along dimension 0, may hold values from 64 to 512
Outputs:
- image_out: bfloat16 [8, 4096, 3072], P('batch', 'seq', 'head'), parts along dimension 0
There are 4 independent parts, one for each index of `batch`. A program takes and returns all parts, laid end to end along the dimension named above; an argument that names none is the same for every part. Nothing has to cross between parts.
Inputs may be any that keep to these rules, and one draw needn't show every extreme that they name: `patch_of`: A permutation: every image band sits on exactly one index of seq. `refresh`: exactly 4 entries are 1, the rest 0.
All inputs are finite; a program needn't handle non-finite values.
Results may differ from a plain program's by a relative error of at most 0.012.
The roundings to bfloat16 on the way count: a program that leaves them out, or rounds other values in their place, can miss the bound.
Values may be sent and summed in bfloat16 or wider, within the bound.
A program may use at most 192 MiB of HBM per device.

v0:
```python
import jax
import jax.numpy as jnp
from jax import lax
from jax.sharding import PartitionSpec as P

GRID_W = 64


epsilon = 1e-06


def in_one_piece(arrays, axis, dim, along):
    both = jnp.concatenate(arrays, axis=along)
    filled, at, done = (lax.all_gather(both, axis, axis=dim, tiled=True), 0, [])
    for a in arrays:
        done.append(lax.slice_in_dim(filled, at, at + a.shape[along], axis=along))
        at += a.shape[along]
    return tuple(done)


def cut_along(array, dim, length):
    dims = array.shape
    pieces = array.reshape(*dims[:dim], length, dims[dim] // length, *dims[dim + 1 :])
    return jnp.moveaxis(pieces, dim, 0)


def sum_at_owner(array, axis, dim):
    pieces = cut_along(array, dim, lax.axis_size(axis))
    arrived = lax.all_to_all(pieces, axis, split_axis=0, concat_axis=0, tiled=True)
    return arrived.astype(jnp.float32).sum(axis=0)


def rotary_tables(raster, head_dim, grid_width):
    half_dim = head_dim // 2
    first_pairs = head_dim // 16
    axis_pairs = (half_dim - first_pairs) // 2
    pair_index = jnp.arange(half_dim, dtype=jnp.int32)
    pair_local = jnp.where(
        pair_index < first_pairs + axis_pairs,
        pair_index - first_pairs,
        pair_index - first_pairs - axis_pairs,
    )
    exponent = -pair_local.astype(jnp.float32) / float(axis_pairs)
    frequency = jnp.where(
        pair_index < first_pairs, jnp.float32(0.0), jnp.power(jnp.float32(10000.0), exponent)
    )
    row_pos = (raster // grid_width).astype(jnp.float32)
    col_pos = (raster % grid_width).astype(jnp.float32)
    position = jnp.where(
        pair_index[None, :] < first_pairs + axis_pairs, row_pos[:, None], col_pos[:, None]
    )
    angles = position * frequency[None, :]
    cosine = jnp.cos(angles)
    sine = jnp.sin(angles)
    return (jnp.concatenate([cosine, cosine], axis=-1), jnp.concatenate([-sine, sine], axis=-1))


def rms_rotate(vectors, gain_vec, cos_full, sin_full):
    scaled = (
        vectors
        * lax.rsqrt(jnp.mean(vectors * vectors, axis=-1, keepdims=True) + epsilon)
        * gain_vec
    )
    half_dim = vectors.shape[-1] // 2
    return (
        scaled * cos_full[None, :, None, :]
        + jnp.roll(scaled, half_dim, axis=-1) * sin_full[None, :, None, :]
    )


def per_device(
    image_hidden,
    modulation,
    qkv_weight,
    out_weight,
    q_gain,
    k_gain,
    text_keys,
    text_values,
    stale_keys,
    stale_values,
    cached_residual,
    patch_of,
    refresh,
    text_len,
):
    prompts, tok_rows, width_part = image_hidden.shape
    head_dim = q_gain.shape[0]
    channels = out_weight.shape[0]
    local_heads = channels // head_dim
    seq_seat = lax.axis_index("seq")
    head_seat = lax.axis_index("head")
    gathered = lax.all_gather(image_hidden, "head", axis=2, tiled=True)
    model_width = gathered.shape[2]
    hidden_f32 = gathered.astype(jnp.float32)
    row_mean = jnp.mean(hidden_f32, axis=-1, keepdims=True)
    centered = hidden_f32 - row_mean
    variance = jnp.mean(centered * centered, axis=-1, keepdims=True)
    normed = centered * lax.rsqrt(variance + epsilon)
    modulated = (
        normed * (1.0 + modulation[:, 1][:, None, :]) + modulation[:, 0][:, None, :]
    ).astype(jnp.bfloat16)
    projected = jnp.dot(
        modulated.reshape(prompts * tok_rows, model_width),
        qkv_weight.reshape(model_width, 3 * channels),
        preferred_element_type=jnp.float32,
    )
    projected = projected.reshape(prompts, tok_rows, 3, local_heads, head_dim)
    seat_ids = jnp.arange(patch_of.shape[0], dtype=jnp.int32)
    own_band = jnp.sum(jnp.where(seat_ids == seq_seat, patch_of, 0))
    own_flag = jnp.sum(jnp.where(seat_ids == seq_seat, refresh, 0))
    raster = own_band * tok_rows + jnp.arange(tok_rows, dtype=jnp.int32)
    cos_full, sin_full = rotary_tables(raster, head_dim, GRID_W)
    fresh_q = rms_rotate(projected[:, :, 0], q_gain, cos_full, sin_full).astype(jnp.bfloat16)
    fresh_k = rms_rotate(projected[:, :, 1], k_gain, cos_full, sin_full).astype(jnp.bfloat16)
    fresh_v = projected[:, :, 2].astype(jnp.bfloat16)
    fresh_k_flat = fresh_k.reshape(prompts, tok_rows, channels)
    fresh_v_flat = fresh_v.reshape(prompts, tok_rows, channels)
    score_scale = head_dim ** (-0.5)
    text_k, text_v = in_one_piece((text_keys, text_values), "seq", 1, 0)
    total_text = text_k.shape[1]
    text_key_rows = text_k.reshape(prompts, total_text, local_heads, head_dim)
    text_value_rows = text_v.reshape(prompts, total_text, local_heads, head_dim)
    text_scores = (
        jnp.einsum("pqhd,pkhd->phqk", fresh_q, text_key_rows, preferred_element_type=jnp.float32)
        * score_scale
    )
    text_valid = jnp.arange(total_text, dtype=jnp.int32)[None, :] < text_len[:, None]
    text_scores = jnp.where(text_valid[:, None, None, :], text_scores, -1e30)
    row_top = jnp.max(text_scores, axis=-1)
    text_weights = jnp.exp(text_scores - row_top[..., None])
    row_total = jnp.sum(text_weights, axis=-1)
    weighted = jnp.einsum(
        "phqk,pkhd->phqd",
        text_weights.astype(jnp.bfloat16),
        text_value_rows,
        preferred_element_type=jnp.float32,
    )
    running = (row_top, row_total, weighted)
    chosen_k = jnp.where(own_flag == 1, fresh_k_flat, stale_keys)
    chosen_v = jnp.where(own_flag == 1, fresh_v_flat, stale_values)
    key_rows = lax.all_gather(chosen_k[None], "seq", axis=0, tiled=True)
    value_rows = lax.all_gather(chosen_v[None], "seq", axis=0, tiled=True)
    piece_count = key_rows.shape[0]
    is_mine = jnp.arange(piece_count, dtype=jnp.int32) == seq_seat
    key_rows = jnp.where(is_mine[:, None, None, None], fresh_k_flat[None], key_rows)
    value_rows = jnp.where(is_mine[:, None, None, None], fresh_v_flat[None], value_rows)
    key_rows = key_rows.reshape(piece_count, prompts, tok_rows, local_heads, head_dim)
    value_rows = value_rows.reshape(piece_count, prompts, tok_rows, local_heads, head_dim)
    old_top, old_total, old_weighted = running
    scores = (
        jnp.einsum("pqhd,npkhd->phqnk", fresh_q, key_rows, preferred_element_type=jnp.float32)
        * score_scale
    )
    new_top = jnp.maximum(old_top, jnp.max(scores, axis=(3, 4)))
    shrink = jnp.exp(old_top - new_top)
    weights = jnp.exp(scores - new_top[..., None, None])
    new_total = old_total * shrink + jnp.sum(weights, axis=(3, 4))
    added = jnp.einsum(
        "phqnk,npkhd->phqd",
        weights.astype(jnp.bfloat16),
        value_rows,
        preferred_element_type=jnp.float32,
    )
    running = (new_top, new_total, old_weighted * shrink[..., None] + added)
    final_top, final_total, final_weighted = running
    attended = (final_weighted / final_total[..., None]).astype(jnp.bfloat16)
    partial_value = jnp.einsum(
        "phqd,hde->pqe",
        attended,
        out_weight.reshape(local_heads, head_dim, model_width),
        preferred_element_type=jnp.float32,
    )
    reduced = sum_at_owner(partial_value.astype(jnp.bfloat16), "head", 2)
    gate_part = lax.dynamic_slice_in_dim(modulation[:, 2], head_seat * width_part, width_part, 1)
    result = (
        image_hidden.astype(jnp.float32)
        + gate_part[:, None, :] * reduced
        + cached_residual.astype(jnp.float32)
    )
    return result.astype(jnp.bfloat16)


def solution(mesh):
    in_specs = (
        P("batch", "seq", "head"),
        P("batch", None, None),
        P(None, None, "head"),
        P("head", None),
        P(),
        P(),
        P("batch", "seq", "head"),
        P("batch", "seq", "head"),
        P("batch", "seq", "head"),
        P("batch", "seq", "head"),
        P("batch", "seq", "head"),
        P("batch"),
        P("batch"),
        P("batch"),
    )
    out_specs = P("batch", "seq", "head")
    return jax.shard_map(
        per_device, mesh=mesh, in_specs=in_specs, out_specs=out_specs, check_vma=False
    )
```

profile of v0, /device:TPU:1, one launch (start us, length us, event | category | flops | bytes accessed | tf_op | source)
XLA Modules:
  0.0 393.8 jit_solution(7118068968956228816)
XLA Ops:
  6.5 0.7 all-gather.7.cloned.1.call-update
  7.3 1.0 pad_maximum_fusion.1
  8.3 0.8 copy.41
  9.2 1.3 select_reduce_fusion
  11.1 0.8 fusion.66
  11.9 18.8 %copy.40 = bf16[3072,3,768]{0,2,1:T(8,128)(2,1)} copy(bf16[3072,3,768]{2,0,1:T(8,128)(2,1)} %param.16) | data formatting | bytes 28311552 | tf_op args[2]
  30.7 0.3 fusion.49
  31.1 1.2 copy.50
  32.4 1.2 copy.49
  34.2 26.8 %all-gather.7.cloned.1.call-done = bf16[2,256,3072]{2,1,0:T(8,128)(2,1)} async-done(((bf16[2,256,1536]{2,1,0:T(8,128)(2,1)}), bf16[2,256,3072]{2,1,0:T(8,128)(2,1)}) %all-gather.7.cloned.1.call-update) | async-done | bytes 3145744 | tf_op jit(solution)/shard_map/all_gather | solution.py:93
  61.0 2.5 convert_reduce_fusion
  63.5 0.3 copy-done.1
  63.8 1.0 fusion.11
  64.8 10.8 %fusion.21 = f32[2,256,3,6,128]{1,4,3,2,0:T(8,128)S(1)} fusion(bf16[3,6,128,3072,1]{3,2,1,0,4:T(8,128)(2,1)} %bitcast.83, bf16[2,256,3072]{2,1,0:T(8,128)(2,1)S(1)} %copy-done.1, f32[2,3072]{1,0:T(2,128)S(1)} %get-tuple-element.20, f32[2,3072]{1,0:T(2,128)S(1)} %get-tuple-element.21, f32[2,256]{1,0:T(2,128)S(1)} %add_rsqrt_fusion.2, ...), kind=kOutput, calls=%fused_computation.29 | convolution fusion | flops 7257194496 | bytes 22073344 | tf_op jit(solution)/shard_map/dot_general | solution.py:103
  75.6 0.3 fusion.35
  75.9 1.7 copy-done
  77.7 0.4 fusion.36
  78.3 1.6 copy.51
  80.0 1.3 mul.206
  81.2 3.1 copy.48
  84.3 1.6 copy.47
  86.0 4.6 %broadcast_select_fusion.3 = (bf16[2,256,768]{2,1,0:T(8,128)(2,1)}, bf16[2,256,768]{2,1,0:T(8,128)(2,1)}) fusion(bf16[2,256,768]{2,1,0:T(8,128)(2,1)} %param.22, pred[]{:T(512)S(6)} %eq.22, f32[2,256,768]{2,1,0:T(8,128)} %copy.51, f32[256,768]{1,0:T(8,128)} %copy.50, f32[256,768]{1,0:T(8,128)} %copy.49, f32[768]{0:T(1024)S(1)} %broadcast_bitcast_fusion, ...), kind=kLoop, calls=%fused_computation.60 | loop fusion | flops 2752512 | bytes 8653825 | tf_op jit(solution)/shard_map/jit(_where)/select_n | solution.py:140
  90.9 1.5 slice.70
  92.6 1.0 broadcast_select_fusion.2
  93.7 2.3 copy.52
  96.2 0.4 fusion.32
  96.6 1.5 all-gather.9.cloned.1.call-done
  98.1 6.1 %fusion.63 = (bf16[2,512,768]{2,0,1:T(2,128)(2,1)}, bf16[2,512,768]{2,0,1:T(2,128)(2,1)S(1)}) fusion(bf16[4,512,768]{2,0,1:T(4,128)(2,1)} %all-gather.9.cloned.1.call-done), kind=kLoop, calls=%fused_computation.104 | loop fusion | bytes 6291456 | tf_op jit(solution)/shard_map/slice | solution.py:16
  104.1 4.9 %copy.75 = bf16[2,512,768]{1,2,0:T(8,128)(2,1)} copy(bf16[2,512,768]{2,0,1:T(2,128)(2,1)} %get-tuple-element.13) | data formatting | bytes 3145728
  109.1 3.5 copy.76
  112.6 2.7 fusion.15
  115.3 1.7 fusion.16
  117.1 2.7 fusion.18
  119.7 51.9 %all-gather.11.cloned.1.call-done = bf16[32,256,768]{2,1,0:T(8,128)(2,1)} async-done(((bf16[2,256,768]{2,1,0:T(8,128)(2,1)}), bf16[32,256,768]{2,1,0:T(8,128)(2,1)}) %all-gather.11.cloned.1.call-update) | async-done | bytes 12582928 | tf_op jit(solution)/shard_map/all_gather | solution.py:142
  171.6 16.0 %copy.53 = bf16[32,256,768]{1,2,0:T(8,128)(2,1)} copy(bf16[32,256,768]{2,1,0:T(8,128)(2,1)} %all-gather.11.cloned.1.call-done) | data formatting | bytes 25165824 | tf_op jit(solution)/shard_map/all_gather | solution.py:142
  187.6 58.3 %all-gather.13.cloned.1.call-done = bf16[32,256,768]{2,1,0:T(8,128)(2,1)} async-done(((bf16[2,256,768]{2,1,0:T(8,128)(2,1)}), bf16[32,256,768]{2,1,0:T(8,128)(2,1)}) %all-gather.13.cloned.1.call-update) | async-done | bytes 12582928 | tf_op jit(solution)/shard_map/all_gather | solution.py:143
  246.0 16.6 %copy.57 = bf16[32,256,768]{1,2,0:T(8,128)(2,1)} copy(bf16[32,256,768]{2,1,0:T(8,128)(2,1)} %all-gather.13.cloned.1.call-done) | data formatting | bytes 25165824 | tf_op jit(solution)/shard_map/all_gather | solution.py:143
  262.6 13.8 %broadcast_select_fusion.1 = (bf16[16,2,256,768]{2,3,1,0:T(8,128)(2,1)S(1)}, bf16[16,2,256,768]{2,3,1,0:T(8,128)(2,1)}) fusion(bf16[16,2,256,768]{2,3,1,0:T(8,128)(2,1)} %bitcast.79, pred[16]{0:T(512)(128)(4,1)S(1)} %iota_compare_fusion.1, bf16[2,256,768]{1,2,0:T(8,128)(2,1)S(1)} %copy-done.3, bf16[16,2,256,768]{2,3,1,0:T(8,128)(2,1)} %bitcast.80, ...), kind=kLoop, calls=%fused_computation.11 | loop fusion | flops 12582912 | bytes 51904528 | tf_op jit(solution)/shard_map/jit(_where)/select_n | solution.py:146
  276.4 18.1 %multiply_reduce_fusion = (f32[2,6,256]{2,1,0:T(8,128)S(1)}, f32[2,6,256,16,256]{2,4,3,1,0:T(8,128)}) fusion(bf16[16,2,256,6,128]{2,4,3,1,0:T(8,128)(2,1)S(1)} %bitcast.81, bf16[2,256,6,128]{1,3,2,0:T(8,128)(2,1)S(1)} %fusion.32), kind=kOutput, calls=%fused_computation.1 | convolution fusion | flops 3246388224 | bytes 63713280 | tf_op jit(solution)/shard_map/pqhd,npkhd->phqnk/dot_general | solution.py:152
  294.5 20.2 %fusion = f32[2,6,256]{2,1,0:T(8,128)S(1)} fusion(f32[2,6,256,16,256]{2,4,3,1,0:T(8,128)} %get-tuple-element.30, f32[2,6,256]{2,1,0:T(8,128)S(1)} %max.14), kind=kLoop, calls=%fused_computation.2 | loop fusion | flops 37745664 | bytes 50356224 | tf_op jit(solution)/shard_map/reduce_sum | solution.py:158
  314.7 25.8 %bitcast_convert_fusion = bf16[2,256,3072]{2,1,0:T(8,128)(2,1)S(1)} fusion(bf16[6,128,3072,1]{2,1,0,3:T(8,128)(2,1)} %bitcast.95, f32[2,6,256,128]{3,2,1,0:T(8,128)} %fusion.18, bf16[16,2,256,6,128]{2,4,3,1,0:T(8,128)(2,1)} %bitcast.85, f32[2,6,256,16,256]{2,4,3,1,0:T(8,128)} %get-tuple-element.30, f32[2,6,256]{2,1,0:T(8,128)S(1)} %max.14, ...), kind=kOutput, calls=%fused_computation.20 | convolution fusion | flops 5678039040 | bytes 72388608 | tf_op jit(solution)/shard_map/phqd,hde->pqe/dot_general | solution.py:168
  340.5 1.9 copy.89
  342.5 4.0 %all-to-all-start = ((bf16[2,2,256,1536]{3,2,1,0:T(8,128)(2,1)}), bf16[2,2,256,1536]{3,2,1,0:T(8,128)(2,1)S(1)}, u32[]{:S(2)}, u32[]{:S(2)}) async-start(bf16[2,2,256,1536]{3,2,1,0:T(8,128)(2,1)} %bitcast.84), calls=%async_computation | async-start | bytes 6291456 | tf_op jit(solution)/shard_map/all_to_all | solution.py:29
  346.5 37.1 %all-to-all-done = bf16[2,2,256,1536]{3,2,1,0:T(8,128)(2,1)S(1)} async-done(((bf16[2,2,256,1536]{3,2,1,0:T(8,128)(2,1)}), bf16[2,2,256,1536]{3,2,1,0:T(8,128)(2,1)S(1)}, u32[]{:S(2)}, u32[]{:S(2)}) %all-to-all-start) | async-done | bytes 3145760 | tf_op jit(solution)/shard_map/all_to_all | solution.py:29
  383.6 0.5 convert_reduce_fusion.1
  384.1 0.9 copy-done.2
  385.0 0.5 copy-done.5
  385.5 1.8 add_convert_fusion
  (44 shorter events, 1.4 us)
Async XLA Ops:
  6.5 54.4 %all-gather.7.cloned.1.call-start = ((), (), s32[]{:S(2)}) async-start(), calls=%async_computation.1 | async-start | bytes 4718592 | tf_op jit(solution)/shard_map/all_gather | solution.py:93
  7.3 90.8 %all-gather.9.cloned.1.call-start = ((), (), s32[]{:S(2)}) async-start(), calls=%async_computation.2 | async-start | bytes 3342336 | tf_op jit(solution)/shard_map/all_gather | solution.py:14
  9.1 162.5 %all-gather.11.cloned.1.call-start = ((), (), s32[]{:S(2)}) async-start(), calls=%async_computation.3 | async-start | bytes 13369344 | tf_op jit(solution)/shard_map/all_gather | solution.py:142
  30.7 2.8 copy-start.6
  61.0 2.8 copy-start.1
  75.6 2.1 copy-start
  75.6 2.1 copy-start.8
  80.0 4.4 %slice-start = ((f32[2,256,3,6,128]{1,4,3,2,0:T(8,128)}), f32[2,256,1,6,128]{1,4,3,2,0:T(8,128)S(1)}, s32[]{:S(2)}) async-start(f32[2,256,3,6,128]{1,4,3,2,0:T(8,128)} %copy-done), calls=%async_computation.5 | async-start | bytes 3145728 | tf_op jit(solution)/shard_map/slice | solution.py:115
  90.6 3.0 copy-start.7
  90.6 155.3 %all-gather.13.cloned.1.call-start = ((), (), s32[]{:S(2)}) async-start(), calls=%async_computation.4 | async-start | bytes 13369344 | tf_op jit(solution)/shard_map/all_gather | solution.py:143
  115.3 1.8 copy-start.4
  187.6 75.0 %copy-start.3 = (bf16[2,256,768]{1,2,0:T(8,128)(2,1)S(1)}, bf16[2,256,768]{1,2,0:T(8,128)(2,1)}, u32[]{:S(2)}) copy-start(bf16[2,256,768]{1,2,0:T(8,128)(2,1)} %copy.52) | copy-start | bytes 2359300
  342.5 41.1 %all-to-all-start = ((bf16[2,2,256,1536]{3,2,1,0:T(8,128)(2,1)}), bf16[2,2,256,1536]{3,2,1,0:T(8,128)(2,1)S(1)}, u32[]{:S(2)}, u32[]{:S(2)}) async-start(bf16[2,2,256,1536]{3,2,1,0:T(8,128)(2,1)} %bitcast.84), calls=%async_computation | async-start | bytes 6291456 | tf_op jit(solution)/shard_map/all_to_all | solution.py:29
  383.6 1.4 copy-start.2
  383.6 1.9 copy-start.5
Sparse Core Ops, SparseCore 0:
  9.0 51.9 all-gather.6
  62.7 35.3 all-gather.8
  99.8 71.8 all-gather.10
  173.2 72.7 all-gather.12
where the time goes:
time: 396 us; the launch traced here: 394 us
  waiting for transfers between devices  176 us (44%)
  local copies, waits for them, and re-layouts  86.6 us (22%)
  matrix products  60.1 us (15%)
  other arithmetic  51.9 us (13%)
  between operations  14.6 us (4%)
  starting transfers between devices  4.28 us (1%)
    all_gather x1, waiting for transfers between devices, per_device(): value_rows = lax.all_gather(chosen_v[None], 'seq', axis=0, tiled=True)  58.3 us
    all_gather x1, waiting for transfers between devices, per_device(): key_rows = lax.all_gather(chosen_k[None], 'seq', axis=0, tiled=True)  51.9 us
    all_to_all x1, waiting for transfers between devices, sum_at_owner(): lax.all_to_all(pieces, axis, split_axis=0, concat_axis=0, tiled=True)  37.1 us
    unnamed x21, local copies, waits for them, and re-layouts  30.6 us
    all_gather x1, waiting for transfers between devices, per_device(): gathered = lax.all_gather(image_hidden, 'head', axis=2, tiled=True)  26.8 us
    dot_general x1, matrix products, per_device(): jnp.einsum('phqd,hde->pqe', attended, out_weight.reshape(local_heads, hea...  25.8 us
    reduce_sum x1, other arithmetic, per_device(): new_total = old_total * shrink + jnp.sum(weights, axis=(3, 4))  20.2 us
    dot_general x1, matrix products, per_device(): jnp.einsum('pqhd,npkhd->phqnk', fresh_q, key_rows, preferred_element_type...  18.1 us
  transfers between devices with their start and end apart: 5, of which 5 were waited for; matrix products, arithmetic and copies ran while one was open for 24% of the time, Pallas kernels for 0%

commit v1 on v0

v1 whole, which is shorter than its diff:
```python
import functools
import math

import jax
import jax.numpy as jnp
from jax import lax
from jax.experimental import pallas as pl
from jax.experimental.pallas import tpu as pltpu
from jax.sharding import PartitionSpec as P

GRID_W = 64
EPS = 1e-06
NEG = -1e30
MESH = pl.DeviceIdType.MESH
BF = jnp.bfloat16
F32 = jnp.float32

NC = 4
TRI = 3
RS = 6


def rotary_tables(raster, head_dim, grid_width):
    half_dim = head_dim // 2
    first_pairs = head_dim // 16
    axis_pairs = (half_dim - first_pairs) // 2
    pair_index = jnp.arange(half_dim, dtype=jnp.int32)
    pair_local = jnp.where(
        pair_index < first_pairs + axis_pairs,
        pair_index - first_pairs,
        pair_index - first_pairs - axis_pairs,
    )
    exponent = -pair_local.astype(jnp.float32) / float(axis_pairs)
    frequency = jnp.where(
        pair_index < first_pairs, jnp.float32(0.0), jnp.power(jnp.float32(10000.0), exponent)
    )
    row_pos = (raster // grid_width).astype(jnp.float32)
    col_pos = (raster % grid_width).astype(jnp.float32)
    position = jnp.where(
        pair_index[None, :] < first_pairs + axis_pairs, row_pos[:, None], col_pos[:, None]
    )
    angles = position * frequency[None, :]
    cosine = jnp.cos(angles)
    sine = jnp.sin(angles)
    return (jnp.concatenate([cosine, cosine], axis=-1), jnp.concatenate([-sine, sine], axis=-1))


def kernel(
    nb,
    refresh_ref,
    tlen_ref,
    mod_ref,
    cos_ref,
    sin_ref,
    qg_ref,
    kg_ref,
    x_hbm,
    w_hbm,
    wo_hbm,
    tk_hbm,
    tv_hbm,
    sk_hbm,
    sv_hbm,
    cr_hbm,
    out_hbm,
    w,
    xo,
    xp,
    xm,
    sk,
    sv,
    cr,
    stage,
    fresh,
    rowb,
    kvb,
    textb,
    acc,
    mst,
    lst,
    oown,
    mown,
    lown,
    osend,
    ob,
    attb,
    attp,
    wown,
    woth,
    pacc,
    outv,
    lsem,
    img_s,
    img_r,
    txt_s,
    txt_r,
    ty_s,
    ty_r,
    row_s,
    row_r,
    y_s,
    y_r,
    f_s,
    f_r,
    o_s,
    o_r,
    a_s,
    a_r,
    w_s,
    w_r,
):
    b = lax.axis_index("batch")
    me = lax.axis_index("seq")
    h = lax.axis_index("head")
    k = me % 2
    xl = (me // 2) % 2
    y = me // 4
    mine = me % 4
    half = xo.shape[2]
    width = 2 * half
    cr_rows = xo.shape[1] // NC
    hd = 128
    tw = TRI * hd
    ns = 2 * nb
    wrows = woth.shape[0] // ns
    trow = tk_hbm.shape[1]
    cexp = (hd ** -0.5) * math.log2(math.e)

    def member(rel):
        return ((xl + rel // 2) % 2) * 2 + (k + rel % 2) % 2

    def row_peer(rel):
        return {"seq": y * 4 + member(rel)}

    def y_of(d):
        return (y + d) % 4

    def y_peer(d):
        return {"seq": y_of(d) * 4 + mine}

    partner = {"head": 1 - h}

    def remote(src, dst, ss, rs, dev):
        return pltpu.make_async_remote_copy(src, dst, ss, rs, device_id=dev, device_id_type=MESH)

    local = [
        pltpu.make_async_copy(x_hbm, xo, lsem.at[0]),
        pltpu.make_async_copy(w_hbm.at[0], w.at[0], lsem.at[1]),
        pltpu.make_async_copy(w_hbm.at[1], w.at[1], lsem.at[2]),
        pltpu.make_async_copy(w_hbm.at[2], w.at[2], lsem.at[3]),
        pltpu.make_async_copy(sk_hbm, sk, lsem.at[4]),
        pltpu.make_async_copy(sv_hbm, sv, lsem.at[5]),
        pltpu.make_async_copy(
            wo_hbm.at[:, pl.ds(pl.multiple_of(h * half, 128), half)], wown, lsem.at[6]
        ),
        pltpu.make_async_copy(cr_hbm, cr, lsem.at[7]),
    ]
    for c_ in local:
        c_.start()

    peers = [partner]
    peers += [row_peer(r) for r in (1, 2, 3)]
    peers += [y_peer(d) for d in (1, 2, 3)]
    zpeers = []
    for db in range(nb):
        for dk in range(2):
            if db == 0 and dk == 0:
                continue
            dev = {"batch": (b + db) % nb, "seq": me + dk * (1 - 2 * k)}
            zpeers.append((db, dk, dev))
            if db != 0:
                peers.append(dev)
    bar = pltpu.get_barrier_semaphore()
    for p_ in peers:
        pl.semaphore_signal(bar, inc=1, device_id=p_, device_id_type=MESH)
    pl.semaphore_wait(bar, len(peers))

    def img(c):
        rows = pl.ds(pl.multiple_of(c * cr_rows, cr_rows), cr_rows)
        return remote(x_hbm.at[:, rows], xp.at[:, rows], img_s.at[c], img_r.at[c], partner)

    img(0).start()
    img(1).start()

    def txt(rel, part):
        m = member(rel)
        src = (tk_hbm if part == 0 else tv_hbm).at[
            m // 2, :, pl.ds(pl.multiple_of((m % 2) * tw, 128), tw)
        ]
        dst = textb.at[y, mine, :, pl.ds(part * tw, tw)]
        return src, dst

    def txt_remote(rel, part):
        src, dst = txt(rel, part)
        return remote(src, dst, txt_s.at[rel, part], txt_r.at[rel, part], row_peer(rel))

    def txt_arrival(rel, part):
        landed = textb.at[y, member(rel), :, pl.ds(part * tw, tw)]
        return remote(landed, landed, txt_s.at[rel, part], txt_r.at[rel, part], row_peer(rel))

    own_text = []
    for part in range(2):
        src, dst = txt(0, part)
        cp = pltpu.make_async_copy(src, dst, lsem.at[8 + part])
        cp.start()
        own_text.append(cp)
    for rel in (2, 3, 1):
        for part in range(2):
            txt_remote(rel, part).start()

    def row_send(c, rel):
        m = member(rel)
        return remote(
            stage.at[c, m], rowb.at[mine, c], row_s.at[c, rel], row_r.at[c, rel], row_peer(rel)
        )

    def row_arrival(c, rel):
        m = member(rel)
        return remote(
            rowb.at[m, c], rowb.at[m, c], row_s.at[c, rel], row_r.at[c, rel], row_peer(rel)
        )

    def pair_of(part):
        return pl.ds(2 * ((xl + part) % 2), 2)

    def y_send(c, part, way):
        d = 1 if way == 0 else 3
        return remote(
            rowb.at[pair_of(part), c, :, pl.ds(tw, 2 * tw)],
            kvb.at[y, c, pair_of(part)],
            y_s.at[c, part, way],
            y_r.at[c, part, way],
            y_peer(d),
        )

    def y_arrival(c, part, way):
        d = 3 if way == 0 else 1
        landed = kvb.at[y_of(d), c, pair_of(part)]
        return remote(landed, landed, y_s.at[c, part, way], y_r.at[c, part, way], y_peer(d))

    def fwd(c, part):
        d_from = 3 if part == 0 else 1
        d_to = 1 if part == 0 else 3
        held = kvb.at[y_of(d_from), c, pair_of(part)]
        return remote(held, held, f_s.at[c, part], f_r.at[c, part], y_peer(d_to))

    def fwd_arrival(c, part):
        d_from = 3 if part == 0 else 1
        landed = kvb.at[y_of(2), c, pair_of(part)]
        return remote(landed, landed, f_s.at[c, part], f_r.at[c, part], y_peer(d_from))

    def serve_a(c):
        row_arrival(c, 1).wait_recv()
        for way in range(2):
            y_send(c, 0, way).start()

    def serve_b(c):
        row_arrival(c, 2).wait_recv()
        row_arrival(c, 3).wait_recv()
        for way in range(2):
            y_send(c, 1, way).start()

    def forward_a(c):
        y_arrival(c, 0, 0).wait_recv()
        fwd(c, 0).start()

    def forward_b(c):
        y_arrival(c, 1, 1).wait_recv()
        fwd(c, 1).start()

    flag = refresh_ref[me]
    own_off = pl.multiple_of(h * half, 128)
    part_off = pl.multiple_of((1 - h) * half, 128)

    for c_ in local[:6]:
        c_.wait()

    def qkv_step(c, carry):
        img(c).wait_recv()
        rows = pl.ds(pl.multiple_of(c * cr_rows, cr_rows), cr_rows)
        for p in range(2):
            a = xo[p, rows, :].astype(F32)
            d = xp[p, rows, :].astype(F32)
            total = jnp.sum(a, axis=-1, keepdims=True) + jnp.sum(d, axis=-1, keepdims=True)
            mean = total / width
            a = a - mean
            d = d - mean
            var = (
                jnp.sum(a * a, axis=-1, keepdims=True) + jnp.sum(d * d, axis=-1, keepdims=True)
            ) / width
            inv = lax.rsqrt(var + EPS)
            for i, (v, off) in enumerate(((a, own_off), (d, part_off))):
                scale = 1.0 + mod_ref[1, pl.ds(p, 1), pl.ds(off, half)]
                shift = mod_ref[0, pl.ds(p, 1), pl.ds(off, half)]
                xm[i, pl.ds(p * cr_rows, cr_rows), :] = (v * inv * scale + shift).astype(BF)
        cosv = cos_ref[rows, :]
        sinv = sin_ref[rows, :]
        cosv = jnp.concatenate([cosv, cosv], axis=0)
        sinv = jnp.concatenate([sinv, sinv], axis=0)
        for kind in range(3):
            proj = jnp.dot(
                xm[0], w[kind, pl.ds(own_off, half), :], preferred_element_type=F32
            ) + jnp.dot(xm[1], w[kind, pl.ds(part_off, half), :], preferred_element_type=F32)
            for head in range(2 * TRI):
                t = proj[:, head * hd : (head + 1) * hd]
                if kind < 2:
                    gain = (qg_ref if kind == 0 else kg_ref)[...]
                    ms = jnp.mean(t * t, axis=-1, keepdims=True)
                    t = t * lax.rsqrt(ms + EPS) * gain
                    t = t * cosv + pltpu.roll(t, hd // 2, 1) * sinv
                t = t.astype(BF)
                kk, j = head // TRI, head % TRI
                for p in range(2):
                    m = p * 2 + kk
                    piece = t[p * cr_rows : (p + 1) * cr_rows]
                    if kind == 0:
                        stage[c, m, :, j * hd : (j + 1) * hd] = piece
                    else:
                        fresh[c, m, :, (kind - 1) * tw + j * hd : (kind - 1) * tw + (j + 1) * hd] = (
                            piece
                        )
                        old = (sk if kind == 1 else sv)[p, rows, head * hd : (head + 1) * hd]
                        stage[c, m, :, kind * tw + j * hd : kind * tw + (j + 1) * hd] = jnp.where(
                            flag == 1, piece, old
                        )
        for rel in (2, 3, 1):
            row_send(c, rel).start()

        @pl.when(c + 2 < NC)
        def _():
            img(c + 2).start()

        rowb[mine, c] = stage[c, mine]
        serve_a(c)

        @pl.when(c >= 1)
        def _():
            serve_b(c - 1)
            forward_a(c - 1)

        @pl.when(c >= 2)
        def _():
            forward_b(c - 2)

        return carry

    lax.fori_loop(0, NC, qkv_step, 0)

    for cp in own_text:
        cp.wait()
    for rel in (1, 2, 3):
        for part in range(2):
            txt_arrival(rel, part).wait_recv()

    def ty(d):
        return remote(textb.at[y], textb.at[y], ty_s.at[d - 1], ty_r.at[d - 1], y_peer(d))

    def ty_arrival(d):
        landed = textb.at[y_of(4 - d)]
        return remote(landed, landed, ty_s.at[d - 1], ty_r.at[d - 1], y_peer(4 - d))

    for d in (1, 2, 3):
        ty(d).start()

    def w_slot(db, dk):
        return ((b + nb - db) % nb) * 2 + (k + dk) % 2

    def w_rows(s):
        return pl.ds(pl.multiple_of(s * wrows, wrows), wrows)

    my_rows = w_rows(b * 2 + k)
    w_first = remote(
        wo_hbm.at[my_rows, pl.ds(part_off, half)],
        woth.at[my_rows],
        w_s.at[0],
        w_r.at[0],
        partner,
    )
    w_first.start()

    def update(q, blocks, first, m_old, l_old, a_old):
        scores = []
        for kb, _, mask in blocks:
            s = lax.dot_general(
                q, kb(), (((1,), (1,)), ((), ())), preferred_element_type=F32
            )
            if mask is not None:
                s = jnp.where(mask(s.shape), s, NEG)
            scores.append(s)
        top = scores[0]
        top = jnp.max(top, axis=-1, keepdims=True)
        for s in scores[1:]:
            top = jnp.maximum(top, jnp.max(s, axis=-1, keepdims=True))
        if not first:
            top = jnp.maximum(top, m_old)
        ref = top * cexp
        a_new = None
        l_new = None
        for s, (_, vb, _) in zip(scores, blocks):
            e = jnp.exp2(s * cexp - ref)
            ls = jnp.sum(e, axis=-1, keepdims=True)
            av = jnp.dot(e.astype(BF), vb(), preferred_element_type=F32)
            l_new = ls if l_new is None else l_new + ls
            a_new = av if a_new is None else a_new + av
        if not first:
            shrink = jnp.exp2(m_old * cexp - ref)
            l_new = l_new + l_old * shrink
            a_new = a_new + a_old * shrink
        return top, l_new, a_new

    nrow = NC * cr_rows

    def own_step(m, carry):
        for j in range(TRI):
            q = stage[:, m, :, j * hd : (j + 1) * hd].reshape(nrow, hd)

            def kb():
                return fresh[:, m, :, j * hd : (j + 1) * hd].reshape(nrow, hd)

            def vb():
                return fresh[:, m, :, tw + j * hd : tw + (j + 1) * hd].reshape(nrow, hd)

            top, tot, av = update(q, [(kb, vb, None)], True, None, None, None)
            oown[m, j] = av
            mown[m, j] = jnp.broadcast_to(top, (nrow, hd))
            lown[m, j] = jnp.broadcast_to(tot, (nrow, hd))
        return carry

    lax.fori_loop(0, 4, own_step, 0)

    forward_b(NC - 2)
    serve_b(NC - 1)
    forward_a(NC - 1)

    for d in (1, 2, 3):
        ty_arrival(d).wait_recv()
    tlen = tlen_ref[xl]

    def text_and_row(m, carry):
        for j in range(TRI):
            q = rowb[m, :, :, j * hd : (j + 1) * hd].reshape(nrow, hd)
            blocks = []
            for t in range(2):

                def kb(t=t):
                    return textb[2 * t : 2 * t + 2, :, :, j * hd : (j + 1) * hd].reshape(
                        8 * trow, hd
                    )

                def vb(t=t):
                    return textb[2 * t : 2 * t + 2, :, :, tw + j * hd : tw + (j + 1) * hd].reshape(
                        8 * trow, hd
                    )

                def mask(shape, t=t):
                    return lax.broadcasted_iota(jnp.int32, shape, 1) + t * 8 * trow < tlen

                blocks.append((kb, vb, mask))
            for c in range(NC):

                def kb(c=c):
                    return rowb[:, c, :, tw + j * hd : tw + (j + 1) * hd].reshape(4 * cr_rows, hd)

                def vb(c=c):
                    return rowb[:, c, :, 2 * tw + j * hd : 2 * tw + (j + 1) * hd].reshape(
                        4 * cr_rows, hd
                    )

                def mask(shape):
                    return lax.broadcasted_iota(jnp.int32, shape, 1) // cr_rows != m

                blocks.append((kb, vb, mask))
            top, tot, av = update(q, blocks, True, None, None, None)
            acc[m, j] = av
            mst[m, j] = jnp.broadcast_to(top, (nrow, hd))
            lst[m, j] = jnp.broadcast_to(tot, (nrow, hd))
        return carry

    lax.fori_loop(0, 4, text_and_row, 0)

    forward_b(NC - 1)

    remote(woth.at[my_rows], woth.at[my_rows], w_s.at[0], w_r.at[0], partner).wait_recv()
    for i, (db, dk, dev) in enumerate(zpeers):
        remote(woth.at[my_rows], woth.at[my_rows], w_s.at[1 + i], w_r.at[1 + i], dev).start()

    def far_blocks(ys, j):
        blocks = []
        for c in range(NC):

            def kb(c=c):
                return kvb[ys, c, :, :, j * hd : (j + 1) * hd].reshape(4 * cr_rows, hd)

            def vb(c=c):
                return kvb[ys, c, :, :, tw + j * hd : tw + (j + 1) * hd].reshape(4 * cr_rows, hd)

            blocks.append((kb, vb, None))
        return blocks

    def far(ys, m, last):
        res = []
        for j in range(TRI):
            q = rowb[m, :, :, j * hd : (j + 1) * hd].reshape(nrow, hd)
            top, tot, av = update(
                q, far_blocks(ys, j), False, mst[m, j][:, :1], lst[m, j][:, :1], acc[m, j]
            )
            if last:
                res.append((top, tot, av))
            else:
                acc[m, j] = av
                mst[m, j] = jnp.broadcast_to(top, (nrow, hd))
                lst[m, j] = jnp.broadcast_to(tot, (nrow, hd))
        return res

    def far_step(ys):
        def step(m, carry):
            far(ys, m, False)
            return carry

        lax.fori_loop(0, 4, step, 0)

    for c in range(NC):
        y_arrival(c, 1, 0).wait_recv()
    far_step(y_of(3))
    for c in range(NC):
        y_arrival(c, 0, 1).wait_recv()
    far_step(y_of(1))
    for c in range(NC):
        fwd_arrival(c, 0).wait_recv()
        fwd_arrival(c, 1).wait_recv()

    lane = lax.broadcasted_iota(jnp.int32, (nrow, hd), 1)

    def o_send(rel):
        m = member(rel)
        return remote(osend.at[m], ob.at[mine], o_s.at[rel], o_r.at[rel], row_peer(rel))

    def o_arrival(rel):
        m = member(rel)
        return remote(ob.at[m], ob.at[m], o_s.at[rel], o_r.at[rel], row_peer(rel))

    def last_step(i, carry):
        rel = 3 - i
        m = member(rel)
        stats = jnp.zeros((nrow, hd), F32)
        for j, (top, tot, av) in enumerate(far(y_of(2), m, True)):
            osend[m, :, j * hd : (j + 1) * hd] = (av / tot).astype(BF)
            for idx, val in ((2 * j, top), (2 * j + 1, tot)):
                hi = val.astype(BF).astype(F32)
                rest = val - hi
                mid = rest.astype(BF).astype(F32)
                low = rest - mid
                stats = jnp.where(lane == idx, hi, stats)
                stats = jnp.where(lane == RS + idx, mid, stats)
                stats = jnp.where(lane == 2 * RS + idx, low, stats)
        osend[m, :, tw : tw + hd] = stats.astype(BF)

        @pl.when(rel > 0)
        def _():
            o_send(rel).start()

        return carry

    lax.fori_loop(0, 4, last_step, 0)
    ob[mine] = osend[mine]

    def a_send(m):
        return remote(attb.at[m], attp.at[m], a_s.at[m], a_r.at[m], partner)

    def merge(rel, carry):
        m = member(rel)

        @pl.when(rel > 0)
        def _():
            o_arrival(rel).wait_recv()

        stats = ob[m, :, tw : tw + hd].astype(F32)
        for j in range(TRI):

            def col(idx):
                return (
                    stats[:, idx : idx + 1]
                    + stats[:, RS + idx : RS + idx + 1]
                    + stats[:, 2 * RS + idx : 2 * RS + idx + 1]
                )

            m1, l1 = col(2 * j), col(2 * j + 1)
            m2, l2 = mown[m, j][:, :1], lown[m, j][:, :1]
            top = jnp.maximum(m1, m2)
            w1 = l1 * jnp.exp2((m1 - top) * cexp)
            e2 = jnp.exp2((m2 - top) * cexp)
            den = w1 + l2 * e2
            o1 = ob[m, :, j * hd : (j + 1) * hd].astype(F32)
            attb[m, :, j * hd : (j + 1) * hd] = (
                o1 * (w1 / den) + oown[m, j] * (e2 / den)
            ).astype(BF)
        a_send(m).start()
        return carry

    lax.fori_loop(0, 4, merge, 0)

    local[6].wait()
    local[7].wait()
    for i, (db, dk, dev) in enumerate(zpeers):
        rows = w_rows(w_slot(db, dk))
        remote(woth.at[rows], woth.at[rows], w_s.at[1 + i], w_r.at[1 + i], dev).wait_recv()

    def own_proj(p, carry):
        pacc[p] = jnp.dot(attb[2 * p], wown[0:tw, :], preferred_element_type=F32) + jnp.dot(
            attb[2 * p + 1], wown[tw : 2 * tw, :], preferred_element_type=F32
        )
        return carry

    lax.fori_loop(0, 2, own_proj, 0)

    def finish(i, carry):
        p = (xl + i) % 2
        for kk in range(2):
            m = 2 * p + kk
            remote(attp.at[m], attp.at[m], a_s.at[m], a_r.at[m], partner).wait_recv()
        proj = (
            pacc[p]
            + jnp.dot(attp[2 * p], woth[0:tw, :], preferred_element_type=F32)
            + jnp.dot(attp[2 * p + 1], woth[tw : 2 * tw, :], preferred_element_type=F32)
        )
        gate = mod_ref[2, pl.ds(p, 1), pl.ds(own_off, half)]
        outv[p] = (xo[p].astype(F32) + gate * proj + cr[p].astype(F32)).astype(BF)
        pltpu.make_async_copy(outv.at[p], out_hbm.at[p], lsem.at[10 + i]).start()
        return carry

    lax.fori_loop(0, 2, finish, 0)

    for i in range(2):
        p = (xl + i) % 2
        pltpu.make_async_copy(outv.at[p], out_hbm.at[p], lsem.at[10 + i]).wait()
    for c in range(NC):
        img(c).wait_send()
        for rel in (1, 2, 3):
            row_send(c, rel).wait_send()
        for part in range(2):
            for way in range(2):
                y_send(c, part, way).wait_send()
            fwd(c, part).wait_send()
    for rel in (1, 2, 3):
        for part in range(2):
            txt_remote(rel, part).wait_send()
        o_send(rel).wait_send()
    for d in (1, 2, 3):
        ty(d).wait_send()
    w_first.wait_send()
    for i, (db, dk, dev) in enumerate(zpeers):
        remote(woth.at[my_rows], woth.at[my_rows], w_s.at[1 + i], w_r.at[1 + i], dev).wait_send()
    for m in range(4):
        a_send(m).wait_send()


def per_device(
    nb,
    image_hidden,
    modulation,
    qkv_weight,
    out_weight,
    q_gain,
    k_gain,
    text_keys,
    text_values,
    stale_keys,
    stale_values,
    cached_residual,
    patch_of,
    refresh,
    text_len,
):
    prompts, rows, half = image_hidden.shape
    hd = q_gain.shape[0]
    channels = out_weight.shape[0]
    tw = TRI * hd
    cr_rows = rows // NC
    trow = text_keys.shape[1]
    seat = lax.axis_index("seq")
    seat_ids = jnp.arange(patch_of.shape[0], dtype=jnp.int32)
    own_band = jnp.sum(jnp.where(seat_ids == seat, patch_of, 0))
    raster = own_band * rows + jnp.arange(rows, dtype=jnp.int32)
    cos_full, sin_full = rotary_tables(raster, hd, GRID_W)
    smem = pl.BlockSpec(memory_space=pltpu.SMEM)
    vmem = pl.BlockSpec(memory_space=pltpu.VMEM)
    hbm = pl.BlockSpec(memory_space=pl.ANY)
    dma = pltpu.SemaphoreType.DMA
    ns = 2 * nb
    return pl.pallas_call(
        functools.partial(kernel, nb),
        name="joint",
        out_shape=jax.ShapeDtypeStruct(image_hidden.shape, BF),
        in_specs=[smem, smem] + [vmem] * 5 + [hbm] * 8,
        out_specs=hbm,
        scratch_shapes=[
            pltpu.VMEM((3, 2 * half, channels), BF),
            pltpu.VMEM((prompts, rows, half), BF),
            pltpu.VMEM((prompts, rows, half), BF),
            pltpu.VMEM((2, prompts * cr_rows, half), BF),
            pltpu.VMEM((prompts, rows, channels), BF),
            pltpu.VMEM((prompts, rows, channels), BF),
            pltpu.VMEM((prompts, rows, half), BF),
            pltpu.VMEM((NC, 4, cr_rows, 3 * tw), BF),
            pltpu.VMEM((NC, 4, cr_rows, 2 * tw), BF),
            pltpu.VMEM((4, NC, cr_rows, 3 * tw), BF),
            pltpu.VMEM((4, NC, 4, cr_rows, 2 * tw), BF),
            pltpu.VMEM((4, 4, trow, 2 * tw), BF),
            pltpu.VMEM((4, TRI, rows, hd), F32),
            pltpu.VMEM((4, TRI, rows, hd), F32),
            pltpu.VMEM((4, TRI, rows, hd), F32),
            pltpu.VMEM((4, TRI, rows, hd), F32),
            pltpu.VMEM((4, TRI, rows, hd), F32),
            pltpu.VMEM((4, TRI, rows, hd), F32),
            pltpu.VMEM((4, rows, tw + hd), BF),
            pltpu.VMEM((4, rows, tw + hd), BF),
            pltpu.VMEM((4, rows, tw), BF),
            pltpu.VMEM((4, rows, tw), BF),
            pltpu.VMEM((channels, half), BF),
            pltpu.VMEM((channels, half), BF),
            pltpu.VMEM((prompts, rows, half), F32),
            pltpu.VMEM((prompts, rows, half), BF),
            dma((12,)),
            dma((NC,)),
            dma((NC,)),
            dma((4, 2)),
            dma((4, 2)),
            dma((3,)),
            dma((3,)),
            dma((NC, 4)),
            dma((NC, 4)),
            dma((NC, 2, 2)),
            dma((NC, 2, 2)),
            dma((NC, 2)),
            dma((NC, 2)),
            dma((4,)),
            dma((4,)),
            dma((4,)),
            dma((4,)),
            dma((ns,)),
            dma((ns,)),
        ],
        compiler_params=pltpu.CompilerParams(
            collective_id=0, has_side_effects=True, vmem_limit_bytes=66 * 1024 * 1024 - 2097152
        ),
    )(
        refresh,
        text_len,
        jnp.transpose(modulation, (1, 0, 2)),
        cos_full,
        sin_full,
        q_gain.reshape(1, hd),
        k_gain.reshape(1, hd),
        image_hidden,
        jnp.transpose(qkv_weight, (1, 0, 2)),
        out_weight,
        text_keys,
        text_values,
        stale_keys,
        stale_values,
        cached_residual,
    )


def solution(mesh):
    in_specs = (
        P("batch", "seq", "head"),
        P("batch", None, None),
        P(None, None, "head"),
        P("head", None),
        P(),
        P(),
        P("batch", "seq", "head"),
        P("batch", "seq", "head"),
        P("batch", "seq", "head"),
        P("batch", "seq", "head"),
        P("batch", "seq", "head"),
        P("batch"),
        P("batch"),
        P("batch"),
    )
    out_specs = P("batch", "seq", "head")
    return jax.shard_map(
        functools.partial(per_device, mesh.shape["batch"]),
        mesh=mesh,
        in_specs=in_specs,
        out_specs=out_specs,
        check_vma=False,
    )
```

time: 396 us -> 153 us (0.39)
  waiting for transfers between devices: 176 us -> 0 us
  Pallas kernels: 0 us -> 147 us
  local copies, waits for them, and re-layouts: 86.6 us -> 2.65 us
  matrix products: 60.1 us -> 0 us
  other arithmetic: 51.9 us -> 3.38 us
  between operations: 14.6 us -> 0.68 us
  starting transfers between devices: 4.28 us -> 0 us
    pallas_call x0 -> x1, Pallas kernels: none -> 147 us  [per_device(): pl.pallas_call(functools.partial(kernel, nb), name='joint', out_shape=jax...]
    all_gather x4 -> x0, waiting for transfers between devices: 139 us -> none  [the longest x1 58.3 us: per_device(): value_rows = lax.all_gather(chosen_v[None], 'seq', axis=0, tiled=True)]
    dot_general x5 -> x0, matrix products: 60.1 us -> none  [the longest x1 25.8 us: per_device(): jnp.einsum('phqd,hde->pqe', attended, out_weight.reshape(local_heads, hea...]
    all_to_all x1 -> x0, waiting for transfers between devices: 37.1 us -> none  [sum_at_owner(): lax.all_to_all(pieces, axis, split_axis=0, concat_axis=0, tiled=True)]
    all_gather x2 -> x0, local copies, waits for them, and re-layouts: 32.6 us -> none  [the longest x1 16.6 us: per_device(): value_rows = lax.all_gather(chosen_v[None], 'seq', axis=0, tiled=True)]
    unnamed x21 -> x1, local copies, waits for them, and re-layouts: 30.6 us -> 2.65 us
    reduce_sum x7 -> x1, other arithmetic: 27.6 us -> 1.29 us  [per_device(): own_band = jnp.sum(jnp.where(seat_ids == seat, patch_of, 0))]
    select_n x3 -> x0, other arithmetic: 19.4 us -> none  [the longest x1 13.8 us: per_device(): jnp.where(is_mine[:, None, None, None], fresh_k_flat[None], key_rows)]
  transfers between devices with their start and end apart: 5 -> 0, of which waited for: 5 -> 0; matrix products, arithmetic and copies ran while one was open for 24% -> 0% of each run, Pallas kernels for 0% -> 0%
where the time goes in v1:
time: 153 us
  Pallas kernels  147 us (96%)
  other arithmetic  3.38 us (2%)
  local copies, waits for them, and re-layouts  2.65 us (2%)
    pallas_call x1, Pallas kernels, per_device(): pl.pallas_call(functools.partial(kernel, nb), name='joint', out_shape=jax...  147 us

profile of v1, /device:TPU:1, one launch (start us, length us, event | category | flops | bytes accessed | tf_op | source)
XLA Modules:
  0.0 153.3 jit_solution(7351599481306235857)
XLA Ops:
  0.0 1.3 fusion.11
  2.0 0.5 fusion.2
  2.5 0.8 pad_maximum_fusion.1.sin_ref
  3.3 0.8 pad_maximum_fusion.cos_ref
  4.1 146.5 %joint.1 = bf16[2,256,1536]{2,1,0:T(8,128)(2,1)} custom-call(s32[16]{0:T(128)} %refresh_ref.1, s32[2]{0:T(128)} %tlen_ref.1, f32[3,2,3072]{2,1,0:T(2,128)} %bitcast.5, f32[256,128]{1,0:T(8,128)} %pad_maximum_fusion.cos_ref, f32[256,128]{1,0:T(8,128)} %pad_maximum_fusion.1.sin_ref, f32[1,128]{1,0:T(1,128)} %bitcast.6, f32[1,128]{1,0:T(1,128)} %bitcast.7, ...), custom_call_target="tpu_custom_call" | custom-call | tf_op jit(solution)/shard_map/joint/pallas_call | solution.py:690
  150.6 2.7 %copy.16 = bf16[2,256,1536]{2,1,0:T(8,128)(2,1)} copy(bf16[2,256,1536]{2,1,0:T(8,128)(2,1)} %joint.1) | data formatting | bytes 3145728
  (3 shorter events, 0.0 us)

commit v2 on v0

v2 whole, which is shorter than its diff:
```python
import functools
import math

import jax
import jax.numpy as jnp
from jax import lax
from jax.experimental import pallas as pl
from jax.experimental.pallas import tpu as pltpu
from jax.sharding import PartitionSpec as P

EPS = 1e-06
NEG = -1e30
MESH = pl.DeviceIdType.MESH
BF = jnp.bfloat16
F32 = jnp.float32

NC = 4
TRI = 3


def pair_frequency(head_dim):
    half_dim = head_dim // 2
    first_pairs = head_dim // 16
    axis_pairs = (half_dim - first_pairs) // 2
    pair_index = jnp.arange(half_dim, dtype=jnp.int32)
    pair_local = jnp.where(
        pair_index < first_pairs + axis_pairs,
        pair_index - first_pairs,
        pair_index - first_pairs - axis_pairs,
    )
    exponent = -pair_local.astype(jnp.float32) / float(axis_pairs)
    frequency = jnp.where(
        pair_index < first_pairs, jnp.float32(0.0), jnp.power(jnp.float32(10000.0), exponent)
    )
    return jnp.concatenate([frequency, frequency]).reshape(1, head_dim)


def kernel(
    nb,
    patch_ref,
    refresh_ref,
    tlen_ref,
    mod_ref,
    freq_ref,
    qg_ref,
    kg_ref,
    x_hbm,
    w_hbm,
    wo_hbm,
    tk_hbm,
    tv_hbm,
    sk_hbm,
    sv_hbm,
    cr_hbm,
    out_hbm,
    w,
    xf,
    xo,
    cr,
    xm,
    stb,
    fresh,
    rowb,
    kvb,
    textb,
    acc,
    mst,
    lst,
    osend,
    att,
    wown,
    woth,
    outv,
    lsem,
    img_s,
    img_r,
    sib_s,
    sib_r,
    st_s,
    st_r,
    txt_s,
    txt_r,
    ty_s,
    ty_r,
    y_s,
    y_r,
    f_s,
    f_r,
    a_s,
    a_r,
    w_s,
    w_r,
):
    b = lax.axis_index("batch")
    me = lax.axis_index("seq")
    h = lax.axis_index("head")
    k = me % 2
    xl = (me // 2) % 2
    y = me // 4
    mine = me % 4
    half = xo.shape[2]
    width = 2 * half
    cr_rows = xo.shape[1] // NC
    tile = 4 * cr_rows
    hd = 128
    tw = TRI * hd
    ns = 2 * nb
    wrows = woth.shape[0] // ns
    trow = tk_hbm.shape[1]
    cexp = (hd ** -0.5) * math.log2(math.e)

    def member(rel):
        return ((xl + rel // 2) % 2) * 2 + (k + rel % 2) % 2

    def row_peer(rel, other=0):
        return {"seq": y * 4 + member(rel), "head": (h + other) % 2}

    def y_of(d):
        return (y + d) % 4

    def y_peer(d):
        return {"seq": y_of(d) * 4 + mine}

    partner = {"head": 1 - h}

    def remote(src, dst, ss, rs, dev):
        return pltpu.make_async_remote_copy(src, dst, ss, rs, device_id=dev, device_id_type=MESH)

    def rows_of(c):
        return pl.ds(pl.multiple_of(c * cr_rows, cr_rows), cr_rows)

    def tri_cols(kk):
        return pl.ds(pl.multiple_of(kk * tw, 128), tw)

    own_off = pl.multiple_of(h * half, 128)
    part_off = pl.multiple_of((1 - h) * half, 128)

    local = [
        pltpu.make_async_copy(x_hbm.at[xl], xf.at[h, mine], lsem.at[0]),
        pltpu.make_async_copy(sk_hbm.at[xl, :, tri_cols(k)], stb.at[mine, :, 0:tw], lsem.at[1]),
        pltpu.make_async_copy(
            sv_hbm.at[xl, :, tri_cols(k)], stb.at[mine, :, tw : 2 * tw], lsem.at[2]
        ),
        pltpu.make_async_copy(
            tk_hbm.at[xl, :, tri_cols(k)], textb.at[y, mine, :, 0:tw], lsem.at[3]
        ),
        pltpu.make_async_copy(
            tv_hbm.at[xl, :, tri_cols(k)], textb.at[y, mine, :, tw : 2 * tw], lsem.at[4]
        ),
    ]
    for kind in range(3):
        local.append(
            pltpu.make_async_copy(
                w_hbm.at[kind, :, tri_cols(k)], w.at[:, kind * tw : (kind + 1) * tw], lsem.at[5 + kind]
            )
        )
    late = [
        pltpu.make_async_copy(wo_hbm.at[:, pl.ds(own_off, half)], wown, lsem.at[8]),
        pltpu.make_async_copy(cr_hbm, cr, lsem.at[9]),
        pltpu.make_async_copy(x_hbm, xo, lsem.at[10]),
    ]
    for c_ in local:
        c_.start()

    peers = [row_peer(r, 1) for r in range(4)]
    peers += [row_peer(r) for r in (1, 2, 3)]
    peers += [y_peer(d) for d in (1, 2, 3)]
    zpeers = []
    for db in range(nb):
        for dk in range(2):
            if db == 0 and dk == 0:
                continue
            dev = {"batch": (b + db) % nb, "seq": me + dk * (1 - 2 * k)}
            zpeers.append((db, dk, dev))
            if db != 0:
                peers.append(dev)
    bar = pltpu.get_barrier_semaphore()
    for p_ in peers:
        pl.semaphore_signal(bar, inc=1, device_id=p_, device_id_type=MESH)
    pl.semaphore_wait(bar, len(peers))

    def txt(rel, part):
        m = member(rel)
        return remote(
            (tk_hbm if part == 0 else tv_hbm).at[m // 2, :, tri_cols(m % 2)],
            textb.at[y, mine, :, part * tw : (part + 1) * tw],
            txt_s.at[rel, part],
            txt_r.at[rel, part],
            row_peer(rel),
        )

    def txt_arrival(rel, part):
        landed = textb.at[y, member(rel), :, part * tw : (part + 1) * tw]
        return remote(landed, landed, txt_s.at[rel, part], txt_r.at[rel, part], row_peer(rel))

    def img_peer(kind):
        return row_peer((1, 0, 2, 2)[kind], (0, 1, 0, 1)[kind])

    def img(c, kind):
        p = xl if kind < 2 else 1 - xl
        return remote(
            x_hbm.at[p, rows_of(c)],
            xf.at[h, mine, rows_of(c)],
            img_s.at[c, kind],
            img_r.at[c, kind],
            img_peer(kind),
        )

    def img_landed(c, kind):
        m = member((1, 0, 2, 2)[kind])
        return xf.at[(h + (0, 1, 0, 1)[kind]) % 2, m, rows_of(c)]

    def img_arrival(c, kind):
        d = img_landed(c, kind)
        return remote(d, d, img_s.at[c, kind], img_r.at[c, kind], img_peer(kind))

    def pass_on(c, kind):
        d = img_landed(c, kind)
        return remote(d, d, sib_s.at[c, kind - 1], sib_r.at[c, kind - 1], row_peer(1))

    def pass_arrival(c, kind):
        m = member((1, 1, 3, 3)[kind])
        d = xf.at[(h + (0, 1, 0, 1)[kind]) % 2, m, rows_of(c)]
        return remote(d, d, sib_s.at[c, kind - 1], sib_r.at[c, kind - 1], row_peer(1))

    def stale(c, rel, part):
        m = member(rel)
        return remote(
            (sk_hbm if part == 0 else sv_hbm).at[m // 2, rows_of(c), tri_cols(m % 2)],
            stb.at[mine, rows_of(c), part * tw : (part + 1) * tw],
            st_s.at[c, rel, part],
            st_r.at[c, rel, part],
            row_peer(rel),
        )

    def stale_arrival(c, rel, part):
        d = stb.at[member(rel), rows_of(c), part * tw : (part + 1) * tw]
        return remote(d, d, st_s.at[c, rel, part], st_r.at[c, rel, part], row_peer(rel))

    def send_image(c):
        for kind in (1, 2, 3, 0):
            img(c, kind).start()

    def send_stale(c):
        for rel in (2, 3, 1):
            for part in range(2):
                stale(c, rel, part).start()

    send_image(0)
    for rel in (2, 3, 1):
        for part in range(2):
            txt(rel, part).start()
    send_stale(0)

    def send_chunk(c, carry):
        send_image(c)
        send_stale(c)
        return carry

    lax.fori_loop(1, NC, send_chunk, 0)

    def w_slot(db, dk):
        return ((b + nb - db) % nb) * 2 + (k + dk) % 2

    def w_rows(s):
        return pl.ds(pl.multiple_of(s * wrows, wrows), wrows)

    my_rows = w_rows(b * 2 + k)

    def w_pass(i):
        return remote(
            woth.at[my_rows], woth.at[my_rows], w_s.at[1 + i], w_r.at[1 + i], zpeers[i][2]
        )

    w_first = remote(
        wo_hbm.at[my_rows, pl.ds(part_off, half)],
        woth.at[my_rows],
        w_s.at[0],
        w_r.at[0],
        partner,
    )
    w_first.start()
    for c_ in late:
        c_.start()

    def ty(d):
        return remote(textb.at[y], textb.at[y], ty_s.at[d - 1], ty_r.at[d - 1], y_peer(d))

    def ty_arrival(d):
        landed = textb.at[y_of(4 - d)]
        return remote(landed, landed, ty_s.at[d - 1], ty_r.at[d - 1], y_peer(4 - d))

    for c_ in local:
        c_.wait()
    for rel in (1, 2, 3):
        for part in range(2):
            txt_arrival(rel, part).wait_recv()
    for d in (1, 3, 2):
        ty(d).start()

    def pair_of(part):
        return pl.ds(2 * ((xl + part) % 2), 2)

    def y_send(c, part, way):
        return remote(
            rowb.at[pair_of(part), c, :, tw : 3 * tw],
            kvb.at[y, c, pair_of(part)],
            y_s.at[c, part, way],
            y_r.at[c, part, way],
            y_peer(1 if way == 0 else 3),
        )

    def y_arrival(c, part, way):
        d = 3 if way == 0 else 1
        landed = kvb.at[y_of(d), c, pair_of(part)]
        return remote(landed, landed, y_s.at[c, part, way], y_r.at[c, part, way], y_peer(d))

    def fwd(c, part):
        held = kvb.at[y_of(3 if part == 0 else 1), c, pair_of(part)]
        return remote(
            held, held, f_s.at[c, part], f_r.at[c, part], y_peer(1 if part == 0 else 3)
        )

    def fwd_arrival(c, part):
        landed = kvb.at[y_of(2), c, pair_of(part)]
        return remote(
            landed, landed, f_s.at[c, part], f_r.at[c, part], y_peer(3 if part == 0 else 1)
        )

    def nt(q, kv):
        return lax.dot_general(q, kv, (((1,), (1,)), ((), ())), preferred_element_type=F32)

    def lanes_of(s):
        return [s[:, i : i + hd] for i in range(0, s.shape[1], hd)]

    def fold(parts, op):
        while len(parts) > 1:
            parts = [
                op(parts[i], parts[i + 1]) if i + 1 < len(parts) else parts[i]
                for i in range(0, len(parts), 2)
            ]
        return parts[0]

    def query(cq, j):
        return rowb[:, cq, :, j * hd : (j + 1) * hd].reshape(tile, hd)

    def text_piece(t):
        def piece(q, j):
            span = slice(2 * t, 2 * t + 2)
            nkey = 8 * trow
            kt = textb[span, :, :, j * hd : (j + 1) * hd].reshape(nkey, hd)
            sc = nt(q, kt)
            sc = jnp.where(
                lax.broadcasted_iota(jnp.int32, sc.shape, 1) + t * nkey < tlen_ref[xl], sc, NEG
            )

            def weigh(e):
                vt = textb[span, :, :, tw + j * hd : tw + (j + 1) * hd].reshape(nkey, hd)
                return jnp.dot(e.astype(BF), vt, preferred_element_type=F32)

            return sc, weigh

        return piece

    def own_piece(ck):
        def piece(q, j):
            same = (
                lax.broadcasted_iota(jnp.int32, (tile, tile), 0) // cr_rows
                == lax.broadcasted_iota(jnp.int32, (tile, tile), 1) // cr_rows
            )
            kc = rowb[:, ck, :, tw + j * hd : tw + (j + 1) * hd].reshape(tile, hd)
            kf = fresh[:, ck, :, j * hd : (j + 1) * hd].reshape(tile, hd)
            sc = jnp.where(same, nt(q, kf), nt(q, kc))

            def weigh(e):
                vc = rowb[:, ck, :, 2 * tw + j * hd : 2 * tw + (j + 1) * hd].reshape(tile, hd)
                vf = fresh[:, ck, :, tw + j * hd : tw + (j + 1) * hd].reshape(tile, hd)
                return jnp.dot(
                    jnp.where(same, 0.0, e).astype(BF), vc, preferred_element_type=F32
                ) + jnp.dot(jnp.where(same, e, 0.0).astype(BF), vf, preferred_element_type=F32)

            return sc, weigh

        return piece

    def far_piece(ck, d):
        yy = y_of(d)

        def piece(q, j):
            kc = kvb[yy, ck, :, :, j * hd : (j + 1) * hd].reshape(tile, hd)

            def weigh(e):
                vc = kvb[yy, ck, :, :, tw + j * hd : tw + (j + 1) * hd].reshape(tile, hd)
                return jnp.dot(e.astype(BF), vc, preferred_element_type=F32)

            return nt(q, kc), weigh

        return piece

    def unit(lo, hi, pieces, first=False, then=None):
        def step(cq, carry):
            for j in range(TRI):
                q = query(cq, j)
                got = [p(q, j) for p in pieces]
                top = fold([t for sc, _ in got for t in lanes_of(sc)], jnp.maximum)
                top = jnp.broadcast_to(jnp.max(top, axis=-1, keepdims=True), (tile, hd))
                if not first:
                    old = mst[cq, j]
                    top = jnp.maximum(top, old)
                ref = top * cexp
                sums, av = [], None
                for sc, weigh in got:
                    e = [jnp.exp2(t * cexp - ref) for t in lanes_of(sc)]
                    sums += e
                    add = weigh(jnp.concatenate(e, axis=1))
                    av = add if av is None else av + add
                tot = fold(sums, jnp.add)
                if not first:
                    shrink = jnp.exp2(old * cexp - ref)
                    tot = tot + lst[cq, j] * shrink
                    av = av + acc[cq, j] * shrink
                if then is None:
                    mst[cq, j] = top
                    lst[cq, j] = tot
                    acc[cq, j] = av
                else:
                    then(cq, j, tot, av)
            if then is not None:
                then(cq, None, None, None)
            return carry

        lax.fori_loop(lo, hi, step, 0)

    text = [text_piece(0), text_piece(1)]

    def near(*cks):
        return [far_piece(ck, d) for ck in cks for d in (3, 1)]

    def opp(*cks):
        return [far_piece(ck, 2) for ck in cks]

    lane = lax.broadcasted_iota(jnp.int32, (cr_rows, hd), 1) % (hd // 2)
    col = lax.broadcasted_iota(jnp.int32, (cr_rows, hd), 0).astype(F32)
    freq = freq_ref[...]
    first_pairs = hd // 16
    axis_pairs = (hd // 2 - first_pairs) // 2
    is_row = lane < first_pairs + axis_pairs
    low = lax.broadcasted_iota(jnp.int32, (cr_rows, hd), 1) < hd // 2

    def qkv_step(c, carry):
        for kind in (1, 2, 3):
            img_arrival(c, kind).wait_recv()
            pass_on(c, kind).start()
        img_arrival(c, 0).wait_recv()
        for kind in (1, 2, 3):
            pass_arrival(c, kind).wait_recv()
        rows = rows_of(c)
        for m in range(4):
            a = xf[0, m, rows, :].astype(F32)
            d = xf[1, m, rows, :].astype(F32)
            total = jnp.sum(a, axis=-1, keepdims=True) + jnp.sum(d, axis=-1, keepdims=True)
            mean = total / width
            a = a - mean
            d = d - mean
            var = (
                jnp.sum(a * a, axis=-1, keepdims=True) + jnp.sum(d * d, axis=-1, keepdims=True)
            ) / width
            inv = lax.rsqrt(var + EPS)
            for i, v in enumerate((a, d)):
                scale = 1.0 + mod_ref[1, pl.ds(xl, 1), i * half : (i + 1) * half]
                shift = mod_ref[0, pl.ds(xl, 1), i * half : (i + 1) * half]
                xm[m * cr_rows : (m + 1) * cr_rows, i * half : (i + 1) * half] = (
                    v * inv * scale + shift
                ).astype(BF)
        cosv, sinv = [], []
        for m in range(4):
            row_pos = (patch_ref[y * 4 + m] * NC + c).astype(F32)
            angle = jnp.where(is_row, row_pos, col) * freq
            cosv.append(jnp.cos(angle))
            sine = jnp.sin(angle)
            sinv.append(jnp.where(low, -sine, sine))
        cosv = jnp.concatenate(cosv, axis=0)
        sinv = jnp.concatenate(sinv, axis=0)
        for kind in range(3):
            proj = jnp.dot(
                xm[...], w[:, kind * tw : (kind + 1) * tw], preferred_element_type=F32
            )
            for j in range(TRI):
                t = proj[:, j * hd : (j + 1) * hd]
                if kind < 2:
                    gain = (qg_ref if kind == 0 else kg_ref)[...]
                    ms = jnp.mean(t * t, axis=-1, keepdims=True)
                    t = t * lax.rsqrt(ms + EPS) * gain
                    t = t * cosv + pltpu.roll(t, hd // 2, 1) * sinv
                t = t.astype(BF)
                at = kind * tw + j * hd
                for m in range(4):
                    piece = t[m * cr_rows : (m + 1) * cr_rows]
                    if kind == 0:
                        rowb[m, c, :, at : at + hd] = piece
                    else:
                        fresh[m, c, :, at - tw : at - tw + hd] = piece
        for rel in (1, 2, 3):
            for part in range(2):
                stale_arrival(c, rel, part).wait_recv()
        for m in range(4):
            rowb[m, c, :, tw : 3 * tw] = jnp.where(
                refresh_ref[y * 4 + m] == 1, fresh[m, c], stb[m, rows, :]
            )
        for part, way in ((0, 0), (1, 1), (1, 0), (0, 1)):
            y_send(c, part, way).start()

        @pl.when(c >= 1)
        def _():
            y_arrival(c - 1, 0, 0).wait_recv()
            fwd(c - 1, 0).start()
            y_arrival(c - 1, 1, 1).wait_recv()
            fwd(c - 1, 1).start()
            y_arrival(c - 1, 1, 0).wait_recv()
            y_arrival(c - 1, 0, 1).wait_recv()

        @pl.when(c == 1)
        def _():
            for d in (1, 2, 3):
                ty_arrival(d).wait_recv()
            unit(0, 2, text + [own_piece(0), own_piece(1)], first=True)

        @pl.when(c == 2)
        def _():
            unit(0, 2, near(0, 1))

        return carry

    lax.fori_loop(0, NC, qkv_step, 0)

    w_first.wait_recv()
    for i in range(len(zpeers)):
        w_pass(i).start()

    def opp_wait(c):
        fwd_arrival(c, 0).wait_recv()
        fwd_arrival(c, 1).wait_recv()

    unit(2, 4, text + [own_piece(ck) for ck in range(NC)], first=True)
    opp_wait(0)
    opp_wait(1)
    unit(0, 2, [own_piece(2), own_piece(3)] + opp(0, 1))
    y_arrival(NC - 1, 0, 0).wait_recv()
    fwd(NC - 1, 0).start()
    y_arrival(NC - 1, 1, 1).wait_recv()
    fwd(NC - 1, 1).start()
    unit(2, 4, near(0, 1) + opp(0, 1))
    y_arrival(NC - 1, 1, 0).wait_recv()
    y_arrival(NC - 1, 0, 1).wait_recv()
    unit(0, 4, near(2, 3))
    opp_wait(2)
    opp_wait(3)

    def att_slot(hh, m, c):
        at = pl.multiple_of((c % 2) * cr_rows, cr_rows)
        return att.at[hh, m % 2, c // 2, m // 2, pl.ds(at, cr_rows)]

    def a_send(c, rel, other):
        i = rel * 2 + other
        return remote(
            osend.at[member(rel), c],
            att_slot(h, mine, c),
            a_s.at[c, i],
            a_r.at[c, i],
            row_peer(rel, other),
        )

    def a_arrival(c, rel, other):
        i = rel * 2 + other
        d = att_slot((h + other) % 2, member(rel), c)
        return remote(d, d, a_s.at[c, i], a_r.at[c, i], row_peer(rel, other))

    far_order = ((2, 1), (0, 1), (3, 1), (1, 1), (2, 0), (3, 0), (1, 0))

    def deliver(cq, j, tot, av):
        if j is not None:
            o = (av / jnp.sum(tot, axis=-1, keepdims=True)).astype(BF)
            for m in range(4):
                osend[m, cq, :, j * hd : (j + 1) * hd] = o[m * cr_rows : (m + 1) * cr_rows]
            return
        for rel, other in far_order:
            a_send(cq, rel, other).start()
        at = pl.multiple_of((cq % 2) * cr_rows, cr_rows)
        att[h, k, cq // 2, xl, pl.ds(at, cr_rows)] = osend[mine, cq]

    unit(0, 4, opp(2, 3), then=deliver)

    for c_ in late:
        c_.wait()
    for i, (db, dk, dev) in enumerate(zpeers):
        rows = w_rows(w_slot(db, dk))
        remote(woth.at[rows], woth.at[rows], w_s.at[1 + i], w_r.at[1 + i], dev).wait_recv()

    def out_copy(s, p):
        rows = pl.ds(pl.multiple_of(s * 2 * cr_rows, cr_rows), 2 * cr_rows)
        return pltpu.make_async_copy(outv.at[p, rows], out_hbm.at[p, rows], lsem.at[11 + 2 * s + p])

    def finish(s, carry):
        for rel, other in far_order[::-1]:
            for e in range(2):
                a_arrival(2 * s + e, rel, other).wait_recv()
        proj = None
        for i, wref in enumerate((wown, woth)):
            hh = (h + i) % 2
            for kk in range(2):
                lhs = att[hh, kk, s].reshape(tile, tw)
                part = jnp.dot(
                    lhs, wref[kk * tw : (kk + 1) * tw, :], preferred_element_type=F32
                )
                proj = part if proj is None else proj + part
        rows = pl.ds(pl.multiple_of(s * 2 * cr_rows, cr_rows), 2 * cr_rows)
        for p in range(2):
            gate = mod_ref[2, pl.ds(p, 1), pl.ds(own_off, half)]
            outv[p, rows, :] = (
                xo[p, rows, :].astype(F32)
                + gate * proj[p * 2 * cr_rows : (p + 1) * 2 * cr_rows]
                + cr[p, rows, :].astype(F32)
            ).astype(BF)
            out_copy(s, p).start()
        return carry

    lax.fori_loop(0, 2, finish, 0)

    for s in range(2):
        for p in range(2):
            out_copy(s, p).wait()

    def drain(c, carry):
        for kind in range(4):
            img(c, kind).wait_send()
        for kind in (1, 2, 3):
            pass_on(c, kind).wait_send()
        for rel in (1, 2, 3):
            for part in range(2):
                stale(c, rel, part).wait_send()
        for part in range(2):
            for way in range(2):
                y_send(c, part, way).wait_send()
            fwd(c, part).wait_send()
        for rel, other in far_order:
            a_send(c, rel, other).wait_send()
        return carry

    lax.fori_loop(0, NC, drain, 0)
    for rel in (1, 2, 3):
        for part in range(2):
            txt(rel, part).wait_send()
    for d in (1, 2, 3):
        ty(d).wait_send()
    w_first.wait_send()
    for i in range(len(zpeers)):
        w_pass(i).wait_send()


def per_device(
    nb,
    image_hidden,
    modulation,
    qkv_weight,
    out_weight,
    q_gain,
    k_gain,
    text_keys,
    text_values,
    stale_keys,
    stale_values,
    cached_residual,
    patch_of,
    refresh,
    text_len,
):
    prompts, rows, half = image_hidden.shape
    hd = q_gain.shape[0]
    channels = out_weight.shape[0]
    tw = TRI * hd
    cr_rows = rows // NC
    trow = text_keys.shape[1]
    smem = pl.BlockSpec(memory_space=pltpu.SMEM)
    vmem = pl.BlockSpec(memory_space=pltpu.VMEM)
    hbm = pl.BlockSpec(memory_space=pl.ANY)
    dma = pltpu.SemaphoreType.DMA
    ns = 2 * nb
    return pl.pallas_call(
        functools.partial(kernel, nb),
        name="joint",
        out_shape=jax.ShapeDtypeStruct(image_hidden.shape, BF),
        in_specs=[smem] * 3 + [vmem] * 4 + [hbm] * 8,
        out_specs=hbm,
        scratch_shapes=[
            pltpu.VMEM((2 * half, 3 * tw), BF),
            pltpu.VMEM((2, 4, rows, half), BF),
            pltpu.VMEM((prompts, rows, half), BF),
            pltpu.VMEM((prompts, rows, half), BF),
            pltpu.VMEM((4 * cr_rows, 2 * half), BF),
            pltpu.VMEM((4, rows, 2 * tw), BF),
            pltpu.VMEM((4, NC, cr_rows, 2 * tw), BF),
            pltpu.VMEM((4, NC, cr_rows, 3 * tw), BF),
            pltpu.VMEM((4, NC, 4, cr_rows, 2 * tw), BF),
            pltpu.VMEM((4, 4, trow, 2 * tw), BF),
            pltpu.VMEM((NC, TRI, 4 * cr_rows, hd), F32),
            pltpu.VMEM((NC, TRI, 4 * cr_rows, hd), F32),
            pltpu.VMEM((NC, TRI, 4 * cr_rows, hd), F32),
            pltpu.VMEM((4, NC, cr_rows, tw), BF),
            pltpu.VMEM((2, 2, 2, 2, 2 * cr_rows, tw), BF),
            pltpu.VMEM((channels, half), BF),
            pltpu.VMEM((channels, half), BF),
            pltpu.VMEM((prompts, rows, half), BF),
            dma((15,)),
            dma((NC, 4)),
            dma((NC, 4)),
            dma((NC, 3)),
            dma((NC, 3)),
            dma((NC, 4, 2)),
            dma((NC, 4, 2)),
            dma((4, 2)),
            dma((4, 2)),
            dma((3,)),
            dma((3,)),
            dma((NC, 2, 2)),
            dma((NC, 2, 2)),
            dma((NC, 2)),
            dma((NC, 2)),
            dma((NC, 8)),
            dma((NC, 8)),
            dma((ns,)),
            dma((ns,)),
        ],
        compiler_params=pltpu.CompilerParams(
            collective_id=0, has_side_effects=True, vmem_limit_bytes=66 * 1024 * 1024 - 2097152
        ),
    )(
        patch_of,
        refresh,
        text_len,
        jnp.transpose(modulation, (1, 0, 2)),
        pair_frequency(hd),
        q_gain.reshape(1, hd),
        k_gain.reshape(1, hd),
        image_hidden,
        jnp.transpose(qkv_weight, (1, 0, 2)),
        out_weight,
        text_keys,
        text_values,
        stale_keys,
        stale_values,
        cached_residual,
    )


def solution(mesh):
    in_specs = (
        P("batch", "seq", "head"),
        P("batch", None, None),
        P(None, None, "head"),
        P("head", None),
        P(),
        P(),
        P("batch", "seq", "head"),
        P("batch", "seq", "head"),
        P("batch", "seq", "head"),
        P("batch", "seq", "head"),
        P("batch", "seq", "head"),
        P("batch"),
        P("batch"),
        P("batch"),
    )
    out_specs = P("batch", "seq", "head")
    return jax.shard_map(
        functools.partial(per_device, mesh.shape["batch"]),
        mesh=mesh,
        in_specs=in_specs,
        out_specs=out_specs,
        check_vma=False,
    )
```

time: 396 us -> 118 us (0.30)
  waiting for transfers between devices: 176 us -> 0 us
  Pallas kernels: 0 us -> 115 us
  local copies, waits for them, and re-layouts: 86.6 us -> 2.65 us
  matrix products: 60.1 us -> 0 us
  other arithmetic: 51.9 us -> 0.6 us
  between operations: 14.6 us -> 0.01 us
  starting transfers between devices: 4.28 us -> 0 us
    all_gather x4 -> x0, waiting for transfers between devices: 139 us -> none  [the longest x1 58.3 us: per_device(): value_rows = lax.all_gather(chosen_v[None], 'seq', axis=0, tiled=True)]
    pallas_call x0 -> x1, Pallas kernels: none -> 115 us  [per_device(): pl.pallas_call(functools.partial(kernel, nb), name='joint', out_shape=jax...]
    dot_general x5 -> x0, matrix products: 60.1 us -> none  [the longest x1 25.8 us: per_device(): jnp.einsum('phqd,hde->pqe', attended, out_weight.reshape(local_heads, hea...]
    all_to_all x1 -> x0, waiting for transfers between devices: 37.1 us -> none  [sum_at_owner(): lax.all_to_all(pieces, axis, split_axis=0, concat_axis=0, tiled=True)]
    all_gather x2 -> x0, local copies, waits for them, and re-layouts: 32.6 us -> none  [the longest x1 16.6 us: per_device(): value_rows = lax.all_gather(chosen_v[None], 'seq', axis=0, tiled=True)]
    unnamed x21 -> x1, local copies, waits for them, and re-layouts: 30.6 us -> 2.65 us
    reduce_sum x7 -> x0, other arithmetic: 27.6 us -> none  [the longest x1 20.2 us: per_device(): new_total = old_total * shrink + jnp.sum(weights, axis=(3, 4))]
    select_n x4 -> x1, other arithmetic: 19.4 us -> 0.01 us  [pair_frequency(): jnp.where(pair_index < first_pairs, jnp.float32(0.0), jnp.power(jnp.float...]
  transfers between devices with their start and end apart: 5 -> 0, of which waited for: 5 -> 0; matrix products, arithmetic and copies ran while one was open for 24% -> 0% of each run, Pallas kernels for 0% -> 0%
where the time goes in v2:
time: 118 us
  Pallas kernels  115 us (97%)
  local copies, waits for them, and re-layouts  2.65 us (2%)
    pallas_call x1, Pallas kernels, per_device(): pl.pallas_call(functools.partial(kernel, nb), name='joint', out_shape=jax...  115 us
    unnamed x1, local copies, waits for them, and re-layouts  2.65 us

profile of v2, /device:TPU:1, one launch (start us, length us, event | category | flops | bytes accessed | tf_op | source)
XLA Modules:
  0.0 118.0 jit_solution(2037596926060987348)
XLA Ops:
  0.0 0.6 maximum_bitcast_fusion.freq_ref
  0.6 114.7 %joint.1 = bf16[2,256,1536]{2,1,0:T(8,128)(2,1)} custom-call(s32[16]{0:T(128)} %patch_ref.1, s32[16]{0:T(128)} %refresh_ref.1, s32[2]{0:T(128)} %tlen_ref.1, f32[3,2,3072]{2,1,0:T(2,128)} %bitcast.7, f32[1,128]{1,0:T(1,128)} %maximum_bitcast_fusion.freq_ref, f32[1,128]{1,0:T(1,128)} %bitcast.8, f32[1,128]{1,0:T(1,128)} %bitcast.9, ...), custom_call_target="tpu_custom_call" | custom-call | tf_op jit(solution)/shard_map/joint/pallas_call | solution.py:688
  115.3 2.7 %copy.16 = bf16[2,256,1536]{2,1,0:T(8,128)(2,1)} copy(bf16[2,256,1536]{2,1,0:T(8,128)(2,1)} %joint.1) | data formatting | bytes 3145728
  (1 shorter events, 0.0 us)

commit v3 on v2

--- a/solution.py
+++ b/solution.py
@@ -3,18 +3,21 @@
 
 import jax
 import jax.numpy as jnp
+import numpy as np
 from jax import lax
 from jax.experimental import pallas as pl
 from jax.experimental.pallas import tpu as pltpu
 from jax.sharding import PartitionSpec as P
 
+GRID_W = 64
 EPS = 1e-06
 NEG = -1e30
 MESH = pl.DeviceIdType.MESH
 BF = jnp.bfloat16
 F32 = jnp.float32
 
-NC = 4
+NC = 8
+NT = 4
 TRI = 3
 
 
@@ -22,17 +25,12 @@
     half_dim = head_dim // 2
     first_pairs = head_dim // 16
     axis_pairs = (half_dim - first_pairs) // 2
-    pair_index = jnp.arange(half_dim, dtype=jnp.int32)
-    pair_local = jnp.where(
-        pair_index < first_pairs + axis_pairs,
-        pair_index - first_pairs,
-        pair_index - first_pairs - axis_pairs,
-    )
-    exponent = -pair_local.astype(jnp.float32) / float(axis_pairs)
-    frequency = jnp.where(
-        pair_index < first_pairs, jnp.float32(0.0), jnp.power(jnp.float32(10000.0), exponent)
-    )
-    return jnp.concatenate([frequency, frequency]).reshape(1, head_dim)
+    pair = np.arange(half_dim)
+    local = np.where(pair < first_pairs + axis_pairs, pair - first_pairs, pair - first_pairs - axis_pairs)
+    exponent = -local.astype(np.float32) / np.float32(axis_pairs)
+    power = np.power(10000.0, exponent.astype(np.float64))
+    frequency = np.where(pair < first_pairs, 0.0, power).astype(np.float32)
+    return np.concatenate([frequency, frequency]).reshape(1, head_dim)
 
 
 def kernel(
@@ -101,7 +99,8 @@
     half = xo.shape[2]
     width = 2 * half
     cr_rows = xo.shape[1] // NC
-    tile = 4 * cr_rows
+    t_rows = xo.shape[1] // NT
+    tile = 4 * t_rows
     hd = 128
     tw = TRI * hd
     ns = 2 * nb
@@ -120,8 +119,6 @@
 
     def y_peer(d):
         return {"seq": y_of(d) * 4 + mine}
-
-    partner = {"head": 1 - h}
 
     def remote(src, dst, ss, rs, dev):
         return pltpu.make_async_remote_copy(src, dst, ss, rs, device_id=dev, device_id_type=MESH)
@@ -162,9 +159,8 @@
     for c_ in local:
         c_.start()
 
-    peers = [row_peer(r, 1) for r in range(4)]
-    peers += [row_peer(r) for r in (1, 2, 3)]
-    peers += [y_peer(d) for d in (1, 2, 3)]
+    peers = [y_peer(d) for d in (2, 1, 3)]
+    peers += [row_peer(r, 1) for r in range(4)]
     zpeers = []
     for db in range(nb):
         for dk in range(2):
@@ -174,6 +170,7 @@
             zpeers.append((db, dk, dev))
             if db != 0:
                 peers.append(dev)
+    peers += [row_peer(r) for r in (1, 2, 3)]
     bar = pltpu.get_barrier_semaphore()
     for p_ in peers:
         pl.semaphore_signal(bar, inc=1, device_id=p_, device_id_type=MESH)
@@ -184,14 +181,14 @@
         return remote(
             (tk_hbm if part == 0 else tv_hbm).at[m // 2, :, tri_cols(m % 2)],
             textb.at[y, mine, :, part * tw : (part + 1) * tw],
-            txt_s.at[rel, part],
-            txt_r.at[rel, part],
+            txt_s.at[rel],
+            txt_r.at[rel],
             row_peer(rel),
         )
 
-    def txt_arrival(rel, part):
-        landed = textb.at[y, member(rel), :, part * tw : (part + 1) * tw]
-        return remote(landed, landed, txt_s.at[rel, part], txt_r.at[rel, part], row_peer(rel))
+    def txt_arrival(rel):
+        landed = textb.at[y, member(rel)]
+        return remote(landed, landed, txt_s.at[rel], txt_r.at[rel], row_peer(rel))
 
     def img_peer(kind):
         return row_peer((1, 0, 2, 2)[kind], (0, 1, 0, 1)[kind])
@@ -201,7 +198,7 @@
         return remote(
             x_hbm.at[p, rows_of(c)],
             xf.at[h, mine, rows_of(c)],
-            img_s.at[c, kind],
+            img_s.at[kind],
             img_r.at[c, kind],
             img_peer(kind),
         )
@@ -212,30 +209,30 @@
 
     def img_arrival(c, kind):
         d = img_landed(c, kind)
-        return remote(d, d, img_s.at[c, kind], img_r.at[c, kind], img_peer(kind))
+        return remote(d, d, img_s.at[kind], img_r.at[c, kind], img_peer(kind))
 
     def pass_on(c, kind):
         d = img_landed(c, kind)
-        return remote(d, d, sib_s.at[c, kind - 1], sib_r.at[c, kind - 1], row_peer(1))
+        return remote(d, d, sib_s.at[kind - 1], sib_r.at[c, kind - 1], row_peer(1))
 
     def pass_arrival(c, kind):
         m = member((1, 1, 3, 3)[kind])
         d = xf.at[(h + (0, 1, 0, 1)[kind]) % 2, m, rows_of(c)]
-        return remote(d, d, sib_s.at[c, kind - 1], sib_r.at[c, kind - 1], row_peer(1))
+        return remote(d, d, sib_s.at[kind - 1], sib_r.at[c, kind - 1], row_peer(1))
 
     def stale(c, rel, part):
         m = member(rel)
         return remote(
             (sk_hbm if part == 0 else sv_hbm).at[m // 2, rows_of(c), tri_cols(m % 2)],
             stb.at[mine, rows_of(c), part * tw : (part + 1) * tw],
-            st_s.at[c, rel, part],
-            st_r.at[c, rel, part],
+            st_s.at[rel],
+            st_r.at[c, rel],
             row_peer(rel),
         )
 
-    def stale_arrival(c, rel, part):
-        d = stb.at[member(rel), rows_of(c), part * tw : (part + 1) * tw]
-        return remote(d, d, st_s.at[c, rel, part], st_r.at[c, rel, part], row_peer(rel))
+    def stale_arrival(c, rel):
+        d = stb.at[member(rel), rows_of(c)]
+        return remote(d, d, st_s.at[rel], st_r.at[c, rel], row_peer(rel))
 
     def send_image(c):
         for kind in (1, 2, 3, 0):
@@ -246,18 +243,16 @@
             for part in range(2):
                 stale(c, rel, part).start()
 
-    send_image(0)
     for rel in (2, 3, 1):
         for part in range(2):
             txt(rel, part).start()
-    send_stale(0)
 
     def send_chunk(c, carry):
         send_image(c)
         send_stale(c)
         return carry
 
-    lax.fori_loop(1, NC, send_chunk, 0)
+    lax.fori_loop(0, NC, send_chunk, 0)
 
     def w_slot(db, dk):
         return ((b + nb - db) % nb) * 2 + (k + dk) % 2
@@ -277,7 +272,7 @@
         woth.at[my_rows],
         w_s.at[0],
         w_r.at[0],
-        partner,
+        row_peer(2, 1),
     )
     w_first.start()
     for c_ in late:
@@ -293,8 +288,7 @@
     for c_ in local:
         c_.wait()
     for rel in (1, 2, 3):
-        for part in range(2):
-            txt_arrival(rel, part).wait_recv()
+        txt_arrival(rel).wait_recv()
     for d in (1, 3, 2):
         ty(d).start()
 
@@ -303,28 +297,28 @@
 
     def y_send(c, part, way):
         return remote(
-            rowb.at[pair_of(part), c, :, tw : 3 * tw],
-            kvb.at[y, c, pair_of(part)],
-            y_s.at[c, part, way],
+            rowb.at[pair_of(part), rows_of(c), tw : 3 * tw],
+            kvb.at[y, pair_of(part), rows_of(c)],
+            y_s.at[part, way],
             y_r.at[c, part, way],
             y_peer(1 if way == 0 else 3),
         )
 
     def y_arrival(c, part, way):
         d = 3 if way == 0 else 1
-        landed = kvb.at[y_of(d), c, pair_of(part)]
-        return remote(landed, landed, y_s.at[c, part, way], y_r.at[c, part, way], y_peer(d))
+        landed = kvb.at[y_of(d), pair_of(part), rows_of(c)]
+        return remote(landed, landed, y_s.at[part, way], y_r.at[c, part, way], y_peer(d))
 
     def fwd(c, part):
-        held = kvb.at[y_of(3 if part == 0 else 1), c, pair_of(part)]
+        held = kvb.at[y_of(3 if part == 0 else 1), pair_of(part), rows_of(c)]
         return remote(
-            held, held, f_s.at[c, part], f_r.at[c, part], y_peer(1 if part == 0 else 3)
+            held, held, f_s.at[part], f_r.at[c, part], y_peer(1 if part == 0 else 3)
         )
 
     def fwd_arrival(c, part):
-        landed = kvb.at[y_of(2), c, pair_of(part)]
+        landed = kvb.at[y_of(2), pair_of(part), rows_of(c)]
         return remote(
-            landed, landed, f_s.at[c, part], f_r.at[c, part], y_peer(3 if part == 0 else 1)
+            landed, landed, f_s.at[part], f_r.at[c, part], y_peer(3 if part == 0 else 1)
         )
 
     def nt(q, kv):
@@ -341,8 +335,11 @@
             ]
         return parts[0]
 
+    def tile_rows(c):
+        return pl.ds(pl.multiple_of(c * t_rows, t_rows), t_rows)
+
     def query(cq, j):
-        return rowb[:, cq, :, j * hd : (j + 1) * hd].reshape(tile, hd)
+        return rowb[:, tile_rows(cq), j * hd : (j + 1) * hd].reshape(tile, hd)
 
     def text_piece(t):
         def piece(q, j):
@@ -365,16 +362,16 @@
     def own_piece(ck):
         def piece(q, j):
             same = (
-                lax.broadcasted_iota(jnp.int32, (tile, tile), 0) // cr_rows
-                == lax.broadcasted_iota(jnp.int32, (tile, tile), 1) // cr_rows
+                lax.broadcasted_iota(jnp.int32, (tile, tile), 0) // t_rows
+                == lax.broadcasted_iota(jnp.int32, (tile, tile), 1) // t_rows
             )
-            kc = rowb[:, ck, :, tw + j * hd : tw + (j + 1) * hd].reshape(tile, hd)
-            kf = fresh[:, ck, :, j * hd : (j + 1) * hd].reshape(tile, hd)
+            kc = rowb[:, tile_rows(ck), tw + j * hd : tw + (j + 1) * hd].reshape(tile, hd)
+            kf = fresh[:, tile_rows(ck), j * hd : (j + 1) * hd].reshape(tile, hd)
             sc = jnp.where(same, nt(q, kf), nt(q, kc))
 
             def weigh(e):
-                vc = rowb[:, ck, :, 2 * tw + j * hd : 2 * tw + (j + 1) * hd].reshape(tile, hd)
-                vf = fresh[:, ck, :, tw + j * hd : tw + (j + 1) * hd].reshape(tile, hd)
+                vc = rowb[:, tile_rows(ck), 2 * tw + j * hd : 2 * tw + (j + 1) * hd].reshape(tile, hd)
+                vf = fresh[:, tile_rows(ck), tw + j * hd : tw + (j + 1) * hd].reshape(tile, hd)
                 return jnp.dot(
                     jnp.where(same, 0.0, e).astype(BF), vc, preferred_element_type=F32
                 ) + jnp.dot(jnp.where(same, e, 0.0).astype(BF), vf, preferred_element_type=F32)
@@ -387,10 +384,10 @@
         yy = y_of(d)
 
         def piece(q, j):
-            kc = kvb[yy, ck, :, :, j * hd : (j + 1) * hd].reshape(tile, hd)
+            kc = kvb[yy, :, tile_rows(ck), j * hd : (j + 1) * hd].reshape(tile, hd)
 
             def weigh(e):
-                vc = kvb[yy, ck, :, :, tw + j * hd : tw + (j + 1) * hd].reshape(tile, hd)
+                vc = kvb[yy, :, tile_rows(ck), tw + j * hd : tw + (j + 1) * hd].reshape(tile, hd)
                 return jnp.dot(e.astype(BF), vc, preferred_element_type=F32)
 
             return nt(q, kc), weigh
@@ -439,6 +436,13 @@
     def opp(*cks):
         return [far_piece(ck, 2) for ck in cks]
 
+    def own(*cks):
+        return [own_piece(ck) for ck in cks]
+
+    def opp_wait(c):
+        fwd_arrival(c, 0).wait_recv()
+        fwd_arrival(c, 1).wait_recv()
+
     lane = lax.broadcasted_iota(jnp.int32, (cr_rows, hd), 1) % (hd // 2)
     col = lax.broadcasted_iota(jnp.int32, (cr_rows, hd), 0).astype(F32)
     freq = freq_ref[...]
@@ -474,8 +478,10 @@
                 ).astype(BF)
         cosv, sinv = [], []
         for m in range(4):
-            row_pos = (patch_ref[y * 4 + m] * NC + c).astype(F32)
-            angle = jnp.where(is_row, row_pos, col) * freq
+            raster = patch_ref[y * 4 + m] * (NC * cr_rows) + c * cr_rows
+            row_pos = (raster // GRID_W).astype(F32)
+            col_pos = (raster % GRID_W).astype(F32) + col
+            angle = jnp.where(is_row, row_pos, col_pos) * freq
             cosv.append(jnp.cos(angle))
             sine = jnp.sin(angle)
             sinv.append(jnp.where(low, -sine, sine))
@@ -497,15 +503,14 @@
                 for m in range(4):
                     piece = t[m * cr_rows : (m + 1) * cr_rows]
                     if kind == 0:
-                        rowb[m, c, :, at : at + hd] = piece
+                        rowb[m, rows, at : at + hd] = piece
                     else:
-                        fresh[m, c, :, at - tw : at - tw + hd] = piece
+                        fresh[m, rows, at - tw : at - tw + hd] = piece
         for rel in (1, 2, 3):
-            for part in range(2):
-                stale_arrival(c, rel, part).wait_recv()
+            stale_arrival(c, rel).wait_recv()
         for m in range(4):
-            rowb[m, c, :, tw : 3 * tw] = jnp.where(
-                refresh_ref[y * 4 + m] == 1, fresh[m, c], stb[m, rows, :]
+            rowb[m, rows, tw : 3 * tw] = jnp.where(
+                refresh_ref[y * 4 + m] == 1, fresh[m, rows, :], stb[m, rows, :]
             )
         for part, way in ((0, 0), (1, 1), (1, 0), (0, 1)):
             y_send(c, part, way).start()
@@ -519,53 +524,56 @@
             y_arrival(c - 1, 1, 0).wait_recv()
             y_arrival(c - 1, 0, 1).wait_recv()
 
-        @pl.when(c == 1)
+        @pl.when(c == 3)
         def _():
             for d in (1, 2, 3):
                 ty_arrival(d).wait_recv()
-            unit(0, 2, text + [own_piece(0), own_piece(1)], first=True)
-
-        @pl.when(c == 2)
+            unit(0, 2, text + own(0, 1), first=True)
+
+        @pl.when(c == 4)
         def _():
             unit(0, 2, near(0, 1))
 
+        @pl.when(c == 5)
+        def _():
+            unit(2, 3, text + own(0, 1, 2), first=True)
+
+        @pl.when(c == 6)
+        def _():
+            w_first.wait_recv()
+            for i in range(len(zpeers)):
+                w_pass(i).start()
+            for e in range(4):
+                opp_wait(e)
+            unit(0, 2, own(2) + opp(0, 1))
+
         return carry
 
     lax.fori_loop(0, NC, qkv_step, 0)
 
-    w_first.wait_recv()
-    for i in range(len(zpeers)):
-        w_pass(i).start()
-
-    def opp_wait(c):
-        fwd_arrival(c, 0).wait_recv()
-        fwd_arrival(c, 1).wait_recv()
-
-    unit(2, 4, text + [own_piece(ck) for ck in range(NC)], first=True)
-    opp_wait(0)
-    opp_wait(1)
-    unit(0, 2, [own_piece(2), own_piece(3)] + opp(0, 1))
+    unit(2, 3, own(3) + near(0, 1) + opp(0, 1))
+    unit(0, 2, own(3) + near(2))
     y_arrival(NC - 1, 0, 0).wait_recv()
     fwd(NC - 1, 0).start()
     y_arrival(NC - 1, 1, 1).wait_recv()
     fwd(NC - 1, 1).start()
-    unit(2, 4, near(0, 1) + opp(0, 1))
     y_arrival(NC - 1, 1, 0).wait_recv()
     y_arrival(NC - 1, 0, 1).wait_recv()
-    unit(0, 4, near(2, 3))
-    opp_wait(2)
-    opp_wait(3)
+    unit(0, 2, near(3))
+    unit(3, 4, text + own(0, 1, 2, 3), first=True)
+    for e in range(4, NC):
+        opp_wait(e)
 
     def att_slot(hh, m, c):
-        at = pl.multiple_of((c % 2) * cr_rows, cr_rows)
-        return att.at[hh, m % 2, c // 2, m // 2, pl.ds(at, cr_rows)]
+        at = pl.multiple_of((c % 2) * t_rows, t_rows)
+        return att.at[hh, m % 2, c // 2, m // 2, pl.ds(at, t_rows)]
 
     def a_send(c, rel, other):
         i = rel * 2 + other
         return remote(
             osend.at[member(rel), c],
             att_slot(h, mine, c),
-            a_s.at[c, i],
+            a_s.at[i],
             a_r.at[c, i],
             row_peer(rel, other),
         )
@@ -573,7 +581,7 @@
     def a_arrival(c, rel, other):
         i = rel * 2 + other
         d = att_slot((h + other) % 2, member(rel), c)
-        return remote(d, d, a_s.at[c, i], a_r.at[c, i], row_peer(rel, other))
+        return remote(d, d, a_s.at[i], a_r.at[c, i], row_peer(rel, other))
 
     far_order = ((2, 1), (0, 1), (3, 1), (1, 1), (2, 0), (3, 0), (1, 0))
 
@@ -581,14 +589,17 @@
         if j is not None:
             o = (av / jnp.sum(tot, axis=-1, keepdims=True)).astype(BF)
             for m in range(4):
-                osend[m, cq, :, j * hd : (j + 1) * hd] = o[m * cr_rows : (m + 1) * cr_rows]
+                osend[m, cq, :, j * hd : (j + 1) * hd] = o[m * t_rows : (m + 1) * t_rows]
             return
         for rel, other in far_order:
             a_send(cq, rel, other).start()
-        at = pl.multiple_of((cq % 2) * cr_rows, cr_rows)
-        att[h, k, cq // 2, xl, pl.ds(at, cr_rows)] = osend[mine, cq]
-
-    unit(0, 4, opp(2, 3), then=deliver)
+        at = pl.multiple_of((cq % 2) * t_rows, t_rows)
+        att[h, k, cq // 2, xl, pl.ds(at, t_rows)] = osend[mine, cq]
+
+    unit(0, 2, opp(2, 3), then=deliver)
+    unit(2, 3, near(2, 3) + opp(2, 3), then=deliver)
+    unit(3, 4, near(0, 1, 2, 3))
+    unit(3, 4, opp(0, 1, 2, 3), then=deliver)
 
     for c_ in late:
         c_.wait()
@@ -597,7 +608,7 @@
         remote(woth.at[rows], woth.at[rows], w_s.at[1 + i], w_r.at[1 + i], dev).wait_recv()
 
     def out_copy(s, p):
-        rows = pl.ds(pl.multiple_of(s * 2 * cr_rows, cr_rows), 2 * cr_rows)
+        rows = pl.ds(pl.multiple_of(s * 2 * t_rows, t_rows), 2 * t_rows)
         return pltpu.make_async_copy(outv.at[p, rows], out_hbm.at[p, rows], lsem.at[11 + 2 * s + p])
 
     def finish(s, carry):
@@ -613,12 +624,12 @@
                     lhs, wref[kk * tw : (kk + 1) * tw, :], preferred_element_type=F32
                 )
                 proj = part if proj is None else proj + part
-        rows = pl.ds(pl.multiple_of(s * 2 * cr_rows, cr_rows), 2 * cr_rows)
+        rows = pl.ds(pl.multiple_of(s * 2 * t_rows, t_rows), 2 * t_rows)
         for p in range(2):
             gate = mod_ref[2, pl.ds(p, 1), pl.ds(own_off, half)]
             outv[p, rows, :] = (
                 xo[p, rows, :].astype(F32)
-                + gate * proj[p * 2 * cr_rows : (p + 1) * 2 * cr_rows]
+                + gate * proj[p * 2 * t_rows : (p + 1) * 2 * t_rows]
                 + cr[p, rows, :].astype(F32)
             ).astype(BF)
             out_copy(s, p).start()
@@ -630,26 +641,22 @@
         for p in range(2):
             out_copy(s, p).wait()
 
-    def drain(c, carry):
-        for kind in range(4):
-            img(c, kind).wait_send()
-        for kind in (1, 2, 3):
-            pass_on(c, kind).wait_send()
-        for rel in (1, 2, 3):
-            for part in range(2):
-                stale(c, rel, part).wait_send()
-        for part in range(2):
-            for way in range(2):
-                y_send(c, part, way).wait_send()
-            fwd(c, part).wait_send()
-        for rel, other in far_order:
-            a_send(c, rel, other).wait_send()
-        return carry
-
-    lax.fori_loop(0, NC, drain, 0)
+    def sent(buf, sem):
+        remote(buf, buf, sem, sem, row_peer(1)).wait_send()
+
+    for kind in range(4):
+        sent(xf.at[0, 0], img_s.at[kind])
+    for kind in range(3):
+        sent(xf.at[0, 0], sib_s.at[kind])
     for rel in (1, 2, 3):
-        for part in range(2):
-            txt(rel, part).wait_send()
+        sent(stb.at[0], st_s.at[rel])
+        sent(textb.at[0, 0], txt_s.at[rel])
+    for part in range(2):
+        for way in range(2):
+            sent(kvb.at[0, 0:2], y_s.at[part, way])
+        sent(kvb.at[0, 0:2], f_s.at[part])
+    for rel, other in far_order:
+        sent(osend.at[0], a_s.at[rel * 2 + other])
     for d in (1, 2, 3):
         ty(d).wait_send()
     w_first.wait_send()
@@ -679,6 +686,7 @@
     channels = out_weight.shape[0]
     tw = TRI * hd
     cr_rows = rows // NC
+    t_rows = rows // NT
     trow = text_keys.shape[1]
     smem = pl.BlockSpec(memory_space=pltpu.SMEM)
     vmem = pl.BlockSpec(memory_space=pltpu.VMEM)
@@ -698,35 +706,35 @@
             pltpu.VMEM((prompts, rows, half), BF),
             pltpu.VMEM((4 * cr_rows, 2 * half), BF),
             pltpu.VMEM((4, rows, 2 * tw), BF),
-            pltpu.VMEM((4, NC, cr_rows, 2 * tw), BF),
-            pltpu.VMEM((4, NC, cr_rows, 3 * tw), BF),
-            pltpu.VMEM((4, NC, 4, cr_rows, 2 * tw), BF),
+            pltpu.VMEM((4, rows, 2 * tw), BF),
+            pltpu.VMEM((4, rows, 3 * tw), BF),
+            pltpu.VMEM((4, 4, rows, 2 * tw), BF),
             pltpu.VMEM((4, 4, trow, 2 * tw), BF),
-            pltpu.VMEM((NC, TRI, 4 * cr_rows, hd), F32),
-            pltpu.VMEM((NC, TRI, 4 * cr_rows, hd), F32),
-            pltpu.VMEM((NC, TRI, 4 * cr_rows, hd), F32),
-            pltpu.VMEM((4, NC, cr_rows, tw), BF),
-            pltpu.VMEM((2, 2, 2, 2, 2 * cr_rows, tw), BF),
+            pltpu.VMEM((NT, TRI, 4 * t_rows, hd), F32),
+            pltpu.VMEM((NT, TRI, 4 * t_rows, hd), F32),
+            pltpu.VMEM((NT, TRI, 4 * t_rows, hd), F32),
+            pltpu.VMEM((4, NT, t_rows, tw), BF),
+            pltpu.VMEM((2, 2, 2, 2, 2 * t_rows, tw), BF),
             pltpu.VMEM((channels, half), BF),
             pltpu.VMEM((channels, half), BF),
             pltpu.VMEM((prompts, rows, half), BF),
             dma((15,)),
+            dma((4,)),
             dma((NC, 4)),
+            dma((3,)),
+            dma((NC, 3)),
+            dma((4,)),
             dma((NC, 4)),
-            dma((NC, 3)),
-            dma((NC, 3)),
-            dma((NC, 4, 2)),
-            dma((NC, 4, 2)),
-            dma((4, 2)),
-            dma((4, 2)),
+            dma((4,)),
+            dma((4,)),
             dma((3,)),
             dma((3,)),
+            dma((2, 2)),
             dma((NC, 2, 2)),
-            dma((NC, 2, 2)),
+            dma((2,)),
             dma((NC, 2)),
-            dma((NC, 2)),
-            dma((NC, 8)),
-            dma((NC, 8)),
+            dma((8,)),
+            dma((NT, 8)),
             dma((ns,)),
             dma((ns,)),
         ],
@@ -738,7 +746,7 @@
         refresh,
         text_len,
         jnp.transpose(modulation, (1, 0, 2)),
-        pair_frequency(hd),
+        jnp.asarray(pair_frequency(hd)),
         q_gain.reshape(1, hd),
         k_gain.reshape(1, hd),
         image_hidden,

time: 118 us -> 107 us (0.907)
  Pallas kernels: 115 us -> 104 us
    pallas_call x1, Pallas kernels: 115 us -> 104 us  [per_device(): pl.pallas_call(functools.partial(kernel, nb), name='joint', out_shape=jax...]
where the time goes in v3:
time: 107 us
  Pallas kernels  104 us (97%)
  local copies, waits for them, and re-layouts  2.65 us (2%)
    pallas_call x1, Pallas kernels, per_device(): pl.pallas_call(functools.partial(kernel, nb), name='joint', out_shape=jax...  104 us
    unnamed x1, local copies, waits for them, and re-layouts  2.65 us

profile of v3, /device:TPU:1, one launch (start us, length us, event | category | flops | bytes accessed | tf_op | source)
XLA Modules:
  0.0 106.7 jit_solution(16504042029316914141)
XLA Ops:
  0.0 104.0 %joint.1 = bf16[2,256,1536]{2,1,0:T(8,128)(2,1)} custom-call(s32[16]{0:T(128)} %patch_ref.1, s32[16]{0:T(128)} %refresh_ref.1, s32[2]{0:T(128)} %tlen_ref.1, f32[3,2,3072]{2,1,0:T(2,128)} %bitcast.5, f32[1,128]{1,0:T(1,128)} %constant.2.clone.freq_ref, f32[1,128]{1,0:T(1,128)} %bitcast.6, f32[1,128]{1,0:T(1,128)} %bitcast.7, bf16[2,256,1536]{2,1,0:T(8,128)(2,1)} %x_hbm.1, ...), custom_call_target="tpu_custom_call" | custom-call | tf_op jit(solution)/shard_map/joint/pallas_call | solution.py:696
  104.0 2.7 %copy.17 = bf16[2,256,1536]{2,1,0:T(8,128)(2,1)} copy(bf16[2,256,1536]{2,1,0:T(8,128)(2,1)} %joint.1) | data formatting | bytes 3145728

commit v4 on v3

--- a/solution.py
+++ b/solution.py
@@ -394,7 +394,7 @@
 
         return piece
 
-    def unit(lo, hi, pieces, first=False, then=None):
+    def unit(lo, hi, pieces, first=False, then=None, mid=None):
         def step(cq, carry):
             for j in range(TRI):
                 q = query(cq, j)
@@ -424,6 +424,8 @@
                     then(cq, j, tot, av)
             if then is not None:
                 then(cq, None, None, None)
+            if mid is not None:
+                pl.when(cq == lo)(lambda: relay(mid))
             return carry
 
         lax.fori_loop(lo, hi, step, 0)
@@ -451,10 +453,16 @@
     is_row = lane < first_pairs + axis_pairs
     low = lax.broadcasted_iota(jnp.int32, (cr_rows, hd), 1) < hd // 2
 
-    def qkv_step(c, carry):
+    def relay(c):
         for kind in (1, 2, 3):
             img_arrival(c, kind).wait_recv()
             pass_on(c, kind).start()
+
+    def qkv_step(c, carry):
+        @pl.when(c < 4)
+        def _():
+            relay(c)
+
         img_arrival(c, 0).wait_recv()
         for kind in (1, 2, 3):
             pass_arrival(c, kind).wait_recv()
@@ -515,6 +523,12 @@
         for part, way in ((0, 0), (1, 1), (1, 0), (0, 1)):
             y_send(c, part, way).start()
 
+        @pl.when(c == 1)
+        def _():
+            for d in (1, 2, 3):
+                ty_arrival(d).wait_recv()
+            unit(0, 1, text + own(0), first=True)
+
         @pl.when(c >= 1)
         def _():
             y_arrival(c - 1, 0, 0).wait_recv()
@@ -526,17 +540,18 @@
 
         @pl.when(c == 3)
         def _():
-            for d in (1, 2, 3):
-                ty_arrival(d).wait_recv()
-            unit(0, 2, text + own(0, 1), first=True)
+            unit(1, 2, text + own(0, 1), first=True)
+            relay(4)
+            unit(0, 1, own(1))
 
         @pl.when(c == 4)
         def _():
-            unit(0, 2, near(0, 1))
+            unit(0, 2, near(0, 1), mid=5)
 
         @pl.when(c == 5)
         def _():
             unit(2, 3, text + own(0, 1, 2), first=True)
+            relay(6)
 
         @pl.when(c == 6)
         def _():
@@ -545,14 +560,14 @@
                 w_pass(i).start()
             for e in range(4):
                 opp_wait(e)
-            unit(0, 2, own(2) + opp(0, 1))
+            unit(0, 2, opp(0, 1), mid=7)
 
         return carry
 
     lax.fori_loop(0, NC, qkv_step, 0)
 
     unit(2, 3, own(3) + near(0, 1) + opp(0, 1))
-    unit(0, 2, own(3) + near(2))
+    unit(0, 2, own(2, 3) + near(2))
     y_arrival(NC - 1, 0, 0).wait_recv()
     fwd(NC - 1, 0).start()
     y_arrival(NC - 1, 1, 1).wait_recv()
@@ -560,7 +575,7 @@
     y_arrival(NC - 1, 1, 0).wait_recv()
     y_arrival(NC - 1, 0, 1).wait_recv()
     unit(0, 2, near(3))
-    unit(3, 4, text + own(0, 1, 2, 3), first=True)
+    unit(3, 4, text + own(0), first=True)
     for e in range(4, NC):
         opp_wait(e)
 
@@ -598,8 +613,8 @@
 
     unit(0, 2, opp(2, 3), then=deliver)
     unit(2, 3, near(2, 3) + opp(2, 3), then=deliver)
-    unit(3, 4, near(0, 1, 2, 3))
-    unit(3, 4, opp(0, 1, 2, 3), then=deliver)
+    unit(3, 4, own(1, 2, 3) + near(0, 1))
+    unit(3, 4, near(2, 3) + opp(0, 1, 2, 3), then=deliver)
 
     for c_ in late:
         c_.wait()

time: 107 us -> 106 us (level)
    pallas_call x1, Pallas kernels: 104 us -> 103 us  [per_device(): pl.pallas_call(functools.partial(kernel, nb), name='joint', out_shape=jax...]
where the time goes in v4:
time: 106 us
  Pallas kernels  103 us (97%)
  local copies, waits for them, and re-layouts  2.65 us (2%)
    pallas_call x1, Pallas kernels, per_device(): pl.pallas_call(functools.partial(kernel, nb), name='joint', out_shape=jax...  103 us
    unnamed x1, local copies, waits for them, and re-layouts  2.65 us

profile of v4, /device:TPU:1, one launch (start us, length us, event | category | flops | bytes accessed | tf_op | source)
XLA Modules:
  0.0 105.5 jit_solution(17425073152858856876)
XLA Ops:
  0.0 102.9 %joint.1 = bf16[2,256,1536]{2,1,0:T(8,128)(2,1)} custom-call(s32[16]{0:T(128)} %patch_ref.1, s32[16]{0:T(128)} %refresh_ref.1, s32[2]{0:T(128)} %tlen_ref.1, f32[3,2,3072]{2,1,0:T(2,128)} %bitcast.5, f32[1,128]{1,0:T(1,128)} %constant.2.clone.freq_ref, f32[1,128]{1,0:T(1,128)} %bitcast.6, f32[1,128]{1,0:T(1,128)} %bitcast.7, bf16[2,256,1536]{2,1,0:T(8,128)(2,1)} %x_hbm.1, ...), custom_call_target="tpu_custom_call" | custom-call | tf_op jit(solution)/shard_map/joint/pallas_call | solution.py:711
  102.9 2.7 %copy.17 = bf16[2,256,1536]{2,1,0:T(8,128)(2,1)} copy(bf16[2,256,1536]{2,1,0:T(8,128)(2,1)} %joint.1) | data formatting | bytes 3145728

commit v5 on v4

--- a/solution.py
+++ b/solution.py
@@ -312,14 +312,12 @@
     def fwd(c, part):
         held = kvb.at[y_of(3 if part == 0 else 1), pair_of(part), rows_of(c)]
         return remote(
-            held, held, f_s.at[part], f_r.at[c, part], y_peer(1 if part == 0 else 3)
+            held, held, f_s.at[part], f_r.at[c], y_peer(1 if part == 0 else 3)
         )
 
-    def fwd_arrival(c, part):
-        landed = kvb.at[y_of(2), pair_of(part), rows_of(c)]
-        return remote(
-            landed, landed, f_s.at[part], f_r.at[c, part], y_peer(3 if part == 0 else 1)
-        )
+    def fwd_arrival(c):
+        landed = kvb.at[y_of(2), :, rows_of(c)]
+        return remote(landed, landed, f_s.at[0], f_r.at[c], y_peer(3))
 
     def nt(q, kv):
         return lax.dot_general(q, kv, (((1,), (1,)), ((), ())), preferred_element_type=F32)
@@ -442,8 +440,7 @@
         return [own_piece(ck) for ck in cks]
 
     def opp_wait(c):
-        fwd_arrival(c, 0).wait_recv()
-        fwd_arrival(c, 1).wait_recv()
+        fwd_arrival(c).wait_recv()
 
     lane = lax.broadcasted_iota(jnp.int32, (cr_rows, hd), 1) % (hd // 2)
     col = lax.broadcasted_iota(jnp.int32, (cr_rows, hd), 0).astype(F32)
@@ -589,14 +586,15 @@
             osend.at[member(rel), c],
             att_slot(h, mine, c),
             a_s.at[i],
-            a_r.at[c, i],
+            a_r.at[c // 2, i],
             row_peer(rel, other),
         )
 
-    def a_arrival(c, rel, other):
+    def a_arrival(s, rel, other):
         i = rel * 2 + other
-        d = att_slot((h + other) % 2, member(rel), c)
-        return remote(d, d, a_s.at[i], a_r.at[c, i], row_peer(rel, other))
+        m = member(rel)
+        d = att.at[(h + other) % 2, m % 2, s, m // 2]
+        return remote(d, d, a_s.at[i], a_r.at[s, i], row_peer(rel, other))
 
     far_order = ((2, 1), (0, 1), (3, 1), (1, 1), (2, 0), (3, 0), (1, 0))
 
@@ -627,18 +625,18 @@
         return pltpu.make_async_copy(outv.at[p, rows], out_hbm.at[p, rows], lsem.at[11 + 2 * s + p])
 
     def finish(s, carry):
-        for rel, other in far_order[::-1]:
-            for e in range(2):
-                a_arrival(2 * s + e, rel, other).wait_recv()
         proj = None
-        for i, wref in enumerate((wown, woth)):
-            hh = (h + i) % 2
-            for kk in range(2):
-                lhs = att[hh, kk, s].reshape(tile, tw)
-                part = jnp.dot(
-                    lhs, wref[kk * tw : (kk + 1) * tw, :], preferred_element_type=F32
-                )
-                proj = part if proj is None else proj + part
+        for rel, other in ((0, 1), (0, 0), (1, 1), (1, 0)):
+            if (rel, other) != (0, 0):
+                a_arrival(s, rel, other).wait_recv()
+            a_arrival(s, rel + 2, other).wait_recv()
+            kk = member(rel) % 2
+            part = jnp.dot(
+                att[(h + other) % 2, kk, s].reshape(tile, tw),
+                (wown, woth)[other][tri_cols(kk), :],
+                preferred_element_type=F32,
+            )
+            proj = part if proj is None else proj + part
         rows = pl.ds(pl.multiple_of(s * 2 * t_rows, t_rows), 2 * t_rows)
         for p in range(2):
             gate = mod_ref[2, pl.ds(p, 1), pl.ds(own_off, half)]
@@ -747,9 +745,9 @@
             dma((2, 2)),
             dma((NC, 2, 2)),
             dma((2,)),
-            dma((NC, 2)),
+            dma((NC,)),
             dma((8,)),
-            dma((NT, 8)),
+            dma((2, 8)),
             dma((ns,)),
             dma((ns,)),
         ],

time: 106 us -> 105 us (level)
  no operation moved by 1% of the time
where the time goes in v5:
time: 105 us
  Pallas kernels  102 us (97%)
  local copies, waits for them, and re-layouts  2.65 us (3%)
    pallas_call x1, Pallas kernels, per_device(): pl.pallas_call(functools.partial(kernel, nb), name='joint', out_shape=jax...  102 us
    unnamed x1, local copies, waits for them, and re-layouts  2.65 us

profile of v5, /device:TPU:1, one launch (start us, length us, event | category | flops | bytes accessed | tf_op | source)
XLA Modules:
  0.0 104.5 jit_solution(9669410714764091577)
XLA Ops:
  0.0 101.9 %joint.1 = bf16[2,256,1536]{2,1,0:T(8,128)(2,1)} custom-call(s32[16]{0:T(128)} %patch_ref.1, s32[16]{0:T(128)} %refresh_ref.1, s32[2]{0:T(128)} %tlen_ref.1, f32[3,2,3072]{2,1,0:T(2,128)} %bitcast.5, f32[1,128]{1,0:T(1,128)} %constant.2.clone.freq_ref, f32[1,128]{1,0:T(1,128)} %bitcast.6, f32[1,128]{1,0:T(1,128)} %bitcast.7, bf16[2,256,1536]{2,1,0:T(8,128)(2,1)} %x_hbm.1, ...), custom_call_target="tpu_custom_call" | custom-call | tf_op jit(solution)/shard_map/joint/pallas_call | solution.py:709
  101.9 2.7 %copy.17 = bf16[2,256,1536]{2,1,0:T(8,128)(2,1)} copy(bf16[2,256,1536]{2,1,0:T(8,128)(2,1)} %joint.1) | data formatting | bytes 3145728
